TPU v7x, 256 devices: a whole 4x4x8 slice. The times are simulated.
256 devices in a mesh: dp: 8 (over z), expert: 8 (over x, core), mp: 4 (over y).
Axes of the slice: x: 4, y: 4, z: 8, core: 2. Of those that a mesh axis runs over, the one named last changes fastest.
Arguments:
- queries: bfloat16 [256, 4096], P('dp', 'expert'), may hold values from -6 to 6
- fresh_entries: bfloat16 [2, 256, 1024], P(None, 'dp', 'expert'), may hold values from -6 to 6
- page_cache: bfloat16 [8, 1024, 2, 256, 128], P('expert', ('dp', 'mp')), may hold values from -6 to 6
- lengths: int32 [256], replicated, may hold values from 2 to 1024, as said below
- page_holder: int32 [256, 4], replicated, may hold values from 0 to 31, as said below
- page_slot: int32 [256, 4], replicated, may hold values from 0 to 31, as said below
- tokens: bfloat16 [256, 4096], P('dp'), may hold values from -6 to 6
- norm_gain: float32 [4096], replicated, may hold values from 0.5 to 1.5
- out_weight: bfloat16 [4096, 4096], P(('expert', 'mp')), may hold values from -0.09375 to 0.09375
- expert_ids: int32 [256, 2], replicated, may hold values from 0 to 7, all different within a row; in each aligned block of 32 rows (0 to 31, 32 to 63, ...) at most 16 rows name the same one
- gate_values: float32 [256, 2], replicated, may hold values from 0.1 to 0.9
- gate_weight: bfloat16 [8, 4096, 8192], P('expert', None, ('dp', 'mp')), may hold values from -0.09375 to 0.09375
- up_weight: bfloat16 [8, 4096, 8192], P('expert', None, ('dp', 'mp')), may hold values from -0.09375 to 0.09375
- down_weight: bfloat16 [8, 8192, 4096], P('expert', ('dp', 'mp')), may hold values from -0.0625 to 0.0625
Outputs:
- layer_output: bfloat16 [256, 4096], P(('dp', 'expert', 'mp'))
Inputs may be any that keep to these rules, and one draw needn't show every extreme that they name: `lengths`: cached positions of each sequence; sequences of one dp index share a most that is a multiple of 256 and is reached by one of them. `page_holder`: number the sequences in aligned blocks of 32; within one block, among the pages whose index has one remainder modulo 4, every holder index occurs exactly 1 times. `page_slot`: no two pages of all sequences share both holder and slot. `expert_ids`: each row names 2 different experts; in each aligned block of 32 rows no expert is named more than 16 times.
All inputs are finite; a program needn't handle non-finite values.
Results may differ from a plain program's by a relative error of at most 0.014.
Values may be sent and summed in bfloat16 or wider, within the bound.
No kernel may reach another device: no remote copies, remote signals or barrier semaphores. Data moves between devices by JAX's collectives and lax.ppermute only.
A program may use at most 64 MiB of HBM per device.

v0:
```python
import math

import jax
import jax.numpy as jnp
from jax import lax
from jax.sharding import PartitionSpec as P

PMAX = 4
CAP = 16


floor_score = -1e30


def joined_along(parts, dim):
    parts = jnp.moveaxis(parts, 0, dim)
    lengths = parts.shape
    return parts.reshape(*lengths[:dim], lengths[dim] * lengths[dim + 1], *lengths[dim + 2 :])


def from_everyone(array, axis):
    count = lax.axis_size(axis)
    return lax.all_to_all(
        jnp.broadcast_to(array[None], (count, *array.shape)), axis, 0, 0, tiled=True
    )


def gathered_copies(array, axis, dim):
    return joined_along(from_everyone(array, axis), dim)


def in_one_piece(arrays, axis, split_dim, concat_dim, along):
    widths = [math.prod(a.shape[along:]) for a in arrays]
    both = jnp.concatenate(
        [a.reshape(*a.shape[:along], w) for a, w in zip(arrays, widths)], axis=along
    )
    out = lax.all_to_all(both, axis, split_axis=split_dim, concat_axis=concat_dim, tiled=True)
    parts = jnp.split(out, [sum(widths[:k]) for k in range(1, len(widths))], axis=along)
    return tuple((b.reshape(*out.shape[:along], *a.shape[along:]) for a, b in zip(arrays, parts)))


def gathered_once(array, axis):
    leaves = jax.tree.leaves(array)
    turns = sorted(range(len(leaves)), key=lambda k: -leaves[k].size)
    width = (1, *leaves[turns[0]].shape)[-1]
    lines = [
        jnp.pad(leaves[k].reshape(-1), (0, -leaves[k].size % width)).reshape(-1, width)
        for k in turns
    ]
    both, at, found = (from_everyone(jnp.concatenate(lines), axis), 0, {})
    for k, line in zip(turns, lines):
        share = both[:, at : at + len(line)].reshape(len(both), -1)
        found[k] = share[:, : leaves[k].size].reshape(-1, *leaves[k].shape)
        at += len(line)
    numbers = iter(range(len(leaves)))
    return jax.tree.map(lambda _: found[next(numbers)], array)


def folded_in_pairs(pieces, combine):
    while len(jax.tree.leaves(pieces)[0]) > 1:
        pieces = jax.vmap(combine)(
            *(jax.tree.map(lambda part: part[side::2], pieces) for side in (0, 1))
        )
    return jax.tree.map(lambda part: part[0], pieces)


def joined_all(array, axis, combine):
    pieces = gathered_once(
        jax.tree.map(
            lambda part, kind: part.astype(kind), array, (jnp.bfloat16, jnp.bfloat16, jnp.bfloat16)
        ),
        axis,
    )
    return folded_in_pairs(
        jax.tree.map(lambda part, own: part.astype(own.dtype), pieces, array), combine
    )


def in_blocks(array, dim, count):
    lengths = array.shape
    parts = array.reshape(*lengths[:dim], count, lengths[dim] // count, *lengths[dim + 1 :])
    return jnp.moveaxis(parts, dim, 0)


def summed_on_arrival(array, axis, dim):
    parts = in_blocks(array, dim, lax.axis_size(axis))
    arrived = lax.all_to_all(parts, axis, split_axis=0, concat_axis=0, tiled=True)
    return arrived.astype(jnp.float32).sum(axis=0)


def padded_to(lines, count):
    spare = -len(lines) % count
    return jnp.pad(lines, [(0, spare)] + [(0, 0)] * (lines.ndim - 1))


def sum_by_parts(array, axes):
    lines = array.reshape(-1, array.shape[-1])
    own = summed_on_arrival(padded_to(lines, lax.axis_size(axes)), axes, 0)
    whole = gathered_copies(own.astype(jnp.bfloat16), axes, 0)
    return whole[: len(lines)].reshape(array.shape).astype(jnp.float32)


def merge_parts(first_part, second_part):
    highest = jnp.maximum(first_part[0], second_part[0])
    left_factor = jnp.exp(first_part[0] - highest)
    right_factor = jnp.exp(second_part[0] - highest)
    totals = first_part[1] * left_factor + second_part[1] * right_factor
    weighted = first_part[2] * left_factor[..., None] + second_part[2] * right_factor[..., None]
    return (highest, totals, weighted)


def body(
    queries,
    fresh_entries,
    page_cache,
    lengths,
    page_holder,
    page_slot,
    tokens,
    norm_gain,
    out_weight,
    expert_ids,
    gate_values,
    gate_weight,
    up_weight,
    down_weight,
):
    highest_precision = lax.Precision.HIGHEST
    batch_groups = lax.axis_size("dp")
    split_count = lax.axis_size("mp")
    expert_count = lax.axis_size("expert")
    group_index = lax.axis_index("dp")
    expert_index = lax.axis_index("expert")
    split_index = lax.axis_index("mp")
    holders = batch_groups * split_count
    my_holder = group_index * split_count + split_index
    sequences = tokens.shape[0]
    kv_heads = page_cache.shape[0]
    own_count = page_cache.shape[1]
    page_rows = page_cache.shape[3]
    head_size = page_cache.shape[4]
    per_pair = own_count // holders
    page_share = PMAX // split_count
    head_groups = queries.shape[1] // (kv_heads * head_size)
    score_scale = head_size ** (-0.5)
    first_mp = split_index == 0

    def arrange(entries):
        shaped = entries.reshape(batch_groups, sequences, page_share, split_count)
        return shaped.transpose(0, 3, 1, 2).reshape(holders, own_count)

    holder_all = arrange(page_holder)
    slot_all = arrange(page_slot)
    ordinal = jnp.arange(own_count, dtype=jnp.int32)
    mine_source = lax.dynamic_index_in_dim(holder_all, my_holder, 0, keepdims=False)
    same_source = (mine_source[None, :] == mine_source[:, None]) & (
        ordinal[None, :] < ordinal[:, None]
    )
    earlier = jnp.sum(same_source.astype(jnp.int32), axis=1)
    recv_index = mine_source * per_pair + earlier
    is_mine = holder_all == my_holder
    ranking = jnp.cumsum(is_mine.astype(jnp.int32), axis=1) - 1
    matches = is_mine[:, :, None] & (
        ranking[:, :, None] == jnp.arange(per_pair, dtype=jnp.int32)[None, None, :]
    )
    pick_slot = jnp.sum(jnp.where(matches, slot_all[:, :, None], 0), axis=1).reshape(-1)
    pick_position = jnp.sum(jnp.where(matches, ordinal[None, :, None], 0), axis=1).reshape(-1)
    query_matrix = queries.reshape(sequences, kv_heads, head_groups, head_size)
    fresh_key = fresh_entries[0].reshape(sequences, kv_heads, head_size)
    fresh_value = (
        fresh_entries[1]
        .reshape(sequences, kv_heads, head_size)
        .astype(jnp.float32)
        .transpose(1, 0, 2)
    )
    own_score = (
        jnp.einsum("skgd,skd->ksg", query_matrix, fresh_key, preferred_element_type=jnp.float32)
        * score_scale
    )
    own_score = jnp.where(first_mp, own_score, floor_score)
    every_query = gathered_copies(queries, "dp", 0)
    owner_index = jnp.arange(holders * per_pair, dtype=jnp.int32) // per_pair
    seq_pick = owner_index // split_count * sequences + pick_position // page_share
    page_pick = pick_position % page_share * split_count + owner_index % split_count
    query_pick = every_query[seq_pick].reshape(-1, kv_heads, head_groups, head_size)
    page_contents = page_cache[:, pick_slot]
    scores = (
        jnp.einsum(
            "nkgd,kntd->kngt",
            query_pick,
            page_contents[:, :, 0],
            preferred_element_type=jnp.float32,
        )
        * score_scale
    )
    position = page_pick[:, None] * page_rows + jnp.arange(page_rows, dtype=jnp.int32)[None, :]
    is_live = (position < lengths[seq_pick][:, None])[None, :, None, :]
    masked = jnp.where(is_live, scores, floor_score)
    page_top = jnp.max(masked, axis=3)
    weights = jnp.where(is_live, jnp.exp(masked - page_top[..., None]), 0.0)
    page_total = jnp.sum(weights, axis=3)
    page_weighted = jnp.einsum(
        "kngt,kntd->kngd",
        weights,
        page_contents[:, :, 1].astype(jnp.float32),
        precision=highest_precision,
    )
    received = tuple(
        (
            part.astype(jnp.float32)
            for part in in_one_piece(
                (
                    page_top.astype(jnp.bfloat16),
                    page_total.astype(jnp.bfloat16),
                    page_weighted.astype(jnp.bfloat16),
                ),
                ("dp", "mp"),
                1,
                1,
                3,
            )
        )
    )
    part_top = received[0][:, recv_index].reshape(kv_heads, sequences, page_share, head_groups)
    part_total = received[1][:, recv_index].reshape(kv_heads, sequences, page_share, head_groups)
    part_weighted = received[2][:, recv_index].reshape(
        kv_heads, sequences, page_share, head_groups, head_size
    )
    highest = jnp.maximum(jnp.max(part_top, axis=2), own_score)
    factor = jnp.exp(part_top - highest[:, :, None, :])
    new_weight = jnp.where(first_mp, jnp.exp(own_score - highest), 0.0)
    totals = jnp.sum(part_total * factor, axis=2) + new_weight
    weighted = (
        jnp.sum(part_weighted * factor[..., None], axis=2)
        + new_weight[..., None] * fresh_value[:, :, None, :]
    )
    merged = joined_all((highest, totals, weighted), "mp", merge_parts)
    attended = (
        (merged[2] / merged[1][..., None])
        .transpose(1, 0, 2, 3)
        .reshape(sequences, -1)
        .astype(jnp.bfloat16)
    )
    head_width = out_weight.shape[0]
    own_heads = lax.dynamic_slice_in_dim(attended, split_index * head_width, head_width, 1)
    partial_value = jnp.dot(own_heads, out_weight, preferred_element_type=jnp.float32)
    summed = sum_by_parts(partial_value.astype(jnp.bfloat16), ("expert", "mp"))
    residual = tokens.astype(jnp.float32) + summed
    normed = (
        residual
        * lax.rsqrt(jnp.mean(residual * residual, axis=-1, keepdims=True) + 1e-05)
        * norm_gain
    ).astype(jnp.bfloat16)
    by_group = expert_ids.reshape(batch_groups, sequences, expert_ids.shape[1])
    shared = jnp.any(by_group[:, :, None, :, None] == by_group[:, None, :, None, :], axis=3)
    before = jnp.arange(sequences)[:, None] < jnp.arange(sequences)[None, :]
    rank_all = jnp.sum((shared & before[None, :, :, None]).astype(jnp.int32), axis=1).reshape(
        expert_ids.shape
    )
    local_experts = gate_weight.shape[0]
    first_expert = expert_index * local_experts
    group_ids = lax.dynamic_slice_in_dim(expert_ids, group_index * sequences, sequences, 0)
    group_ranks = lax.dynamic_slice_in_dim(rank_all, group_index * sequences, sequences, 0)
    expert_range = first_expert + jnp.arange(local_experts, dtype=jnp.int32)
    chooser = (group_ids[None, None] == expert_range[:, None, None, None]) & (
        group_ranks[None, None] == jnp.arange(CAP, dtype=jnp.int32)[None, :, None, None]
    )
    chooser = jnp.sum(chooser.astype(jnp.int32), axis=3).astype(jnp.bfloat16)
    chosen = jnp.einsum("ect,td->ecd", chooser, normed, preferred_element_type=jnp.float32).astype(
        jnp.bfloat16
    )
    piece = gathered_copies(chosen, "dp", 1)
    gate_out = jnp.einsum("erd,edf->erf", piece, gate_weight, preferred_element_type=jnp.float32)
    up_out = jnp.einsum("erd,edf->erf", piece, up_weight, preferred_element_type=jnp.float32)
    hidden = (jax.nn.silu(gate_out) * up_out).astype(jnp.bfloat16)
    own_rows = expert_ids.shape[0] // (batch_groups * expert_count * split_count)
    hidden_grouped = hidden.reshape(local_experts, batch_groups, CAP, hidden.shape[2])
    grouped = jnp.einsum(
        "egcf,efd->gecd", hidden_grouped, down_weight, preferred_element_type=jnp.float32
    ).reshape(batch_groups * local_experts * CAP, -1)
    share_rows = grouped.shape[0] // holders
    summed_rows = summed_on_arrival(grouped.astype(jnp.bfloat16), ("dp", "mp"), 0)
    slot_number = split_index * share_rows + jnp.arange(share_rows, dtype=jnp.int32)
    slot_expert = first_expert + slot_number // CAP
    slot_rank = slot_number % CAP
    group_gates = lax.dynamic_slice_in_dim(gate_values, group_index * sequences, sequences, 0)
    selected = (group_ids[:, :, None] == slot_expert[None, None, :]) & (
        group_ranks[:, :, None] == slot_rank[None, None, :]
    )
    slot_weights = jnp.sum(jnp.where(selected, group_gates[:, :, None], 0.0), axis=1)
    moe = summed_on_arrival(
        jnp.dot(
            slot_weights,
            summed_rows,
            precision=highest_precision,
            preferred_element_type=jnp.float32,
        ).astype(jnp.bfloat16),
        ("expert", "mp"),
        0,
    )
    row_offset = (expert_index * split_count + split_index) * own_rows
    layer_output = lax.dynamic_slice_in_dim(residual, row_offset, own_rows, 0) + moe
    return layer_output.astype(jnp.bfloat16)


def solution(mesh):
    return jax.shard_map(
        body,
        mesh=mesh,
        in_specs=(
            P("dp", "expert"),
            P(None, "dp", "expert"),
            P("expert", ("dp", "mp"), None, None, None),
            P(),
            P(),
            P(),
            P("dp", None),
            P(),
            P(("expert", "mp"), None),
            P(),
            P(),
            P("expert", None, ("dp", "mp")),
            P("expert", None, ("dp", "mp")),
            P("expert", ("dp", "mp"), None),
        ),
        out_specs=P(("dp", "expert", "mp"), None),
        check_vma=False,
    )
```

profile of v0, /device:TPU:8, one launch (start us, length us, event | category | flops | bytes accessed | tf_op | source)
XLA Modules:
  0.0 189.6 jit_solution(10023096029139765574)
XLA Ops:
  0.0 1.6 broadcast_in_dim.55
  1.7 8.6 %all-to-all-start = ((bf16[8,32,512]{2,1,0:T(8,128)(2,1)}), bf16[8,32,512]{2,1,0:T(8,128)(2,1)S(1)}, u32[]{:S(2)}, u32[]{:S(2)}) async-start(bf16[8,32,512]{2,1,0:T(8,128)(2,1)} %broadcast_in_dim.55), calls=%async_computation | async-start | bytes 524288 | tf_op jit(solution)/shard_map/all_to_all | solution.py:23
  15.1 5.2 %gather_fusion.2 = bf16[32,2,256,128]{3,2,1,0:T(8,128)(2,1)} fusion(bf16[32,2,256,128]{3,2,1,0:T(8,128)(2,1)} %bitcast.147, s32[1024]{0:T(1024)S(1)} %pad_clamp_fusion.1), kind=kCustom, calls=%fused_computation.2 | custom fusion | bytes 8388736 | tf_op jit(solution)/shard_map/gather | solution.py:186
  20.4 4.6 %copy.184 = bf16[32,2,256,128]{3,2,0,1:T(8,128)(2,1)} copy(bf16[32,2,256,128]{3,2,1,0:T(8,128)(2,1)} %gather_fusion.2) | data formatting | bytes 8388608 | tf_op jit(solution)/shard_map/gather | solution.py:186
  25.8 2.3 %fusion.67 = (f32[32,4]{1,0:T(8,128)S(1)}, f32[32,4,256]{2,1,0:T(4,128)S(1)}) fusion(bf16[32,4,128]{2,1,0:T(4,128)(2,1)S(1)} %reshape.610, bf16[1,32,2,256,128]{4,3,1,2,0:T(8,128)(2,1)} %bitcast.148, pred[32,256]{1,0:T(8,128)(4,1)S(1)} %add_compare_fusion), kind=kOutput, calls=%fused_computation.145 | convolution fusion | flops 8486784 | bytes 2269696 | tf_op jit(solution)/shard_map/nkgd,kntd->kngt/dot_general | solution.py:188
  28.1 2.6 %fusion.19 = bf16[1,32,4,128]{3,2,1,0:T(4,128)(2,1)S(1)} fusion(bf16[1,32,2,256,128]{4,3,1,2,0:T(8,128)(2,1)} %bitcast.149, f32[32,4,256]{2,1,0:T(4,128)S(1)} %get-tuple-element.32, f32[32,4]{1,0:T(8,128)S(1)} %get-tuple-element.31, pred[32,256]{1,0:T(8,128)(4,1)S(1)} %add_compare_fusion), kind=kOutput, calls=%fused_computation.29 | convolution fusion | flops 50413568 | bytes 2269696 | tf_op jit(solution)/shard_map/kngt,kntd->kngd/dot_general | solution.py:202
  32.2 10.4 %all-to-all-start.1 = ((bf16[1,32,4,130]{3,2,0,1:T(4,128)(2,1)}), bf16[1,32,4,130]{3,2,0,1:T(4,128)(2,1)S(1)}, u32[]{:S(2)}, u32[]{:S(2)}) async-start(bf16[1,32,4,130]{3,2,0,1:T(4,128)(2,1)} %maximum_bitcast_fusion), calls=%async_computation.1 | async-start | bytes 131072 | tf_op jit(solution)/shard_map/all_to_all | solution.py:37
  42.6 8.7 %all-to-all-done.1 = bf16[1,32,4,130]{3,2,0,1:T(4,128)(2,1)S(1)} async-done(((bf16[1,32,4,130]{3,2,0,1:T(4,128)(2,1)}), bf16[1,32,4,130]{3,2,0,1:T(4,128)(2,1)S(1)}, u32[]{:S(2)}, u32[]{:S(2)}) %all-to-all-start.1) | async-done | bytes 33312 | tf_op jit(solution)/shard_map/all_to_all | solution.py:37
  55.0 4.8 %all-to-all-start.2 = ((bf16[4,130,128]{2,1,0:T(8,128)(2,1)}), bf16[4,130,128]{2,1,0:T(8,128)(2,1)S(1)}, u32[]{:S(2)}, u32[]{:S(2)}) async-start(bf16[4,130,128]{2,1,0:T(8,128)(2,1)} %broadcast_in_dim.60), calls=%async_computation.2 | async-start | bytes 278528 | tf_op jit(solution)/shard_map/all_to_all | solution.py:23
  59.8 4.6 %all-to-all-done.2 = bf16[4,130,128]{2,1,0:T(8,128)(2,1)S(1)} async-done(((bf16[4,130,128]{2,1,0:T(8,128)(2,1)}), bf16[4,130,128]{2,1,0:T(8,128)(2,1)S(1)}, u32[]{:S(2)}, u32[]{:S(2)}) %all-to-all-start.2) | async-done | bytes 133152 | tf_op jit(solution)/shard_map/all_to_all | solution.py:23
  67.6 0.9 reshape.712
  68.5 6.5 %all-to-all-start.3 = ((bf16[32,2,2048]{2,1,0:T(2,128)(2,1)}), bf16[32,2,2048]{2,1,0:T(2,128)(2,1)S(1)}, u32[]{:S(2)}, u32[]{:S(2)}) async-start(bf16[32,2,2048]{2,1,0:T(2,128)(2,1)} %reshape.712), calls=%async_computation.3 | async-start | bytes 524288 | tf_op jit(solution)/shard_map/all_to_all | solution.py:87
  75.4 6.8 %all-to-all-done.3 = bf16[32,2,2048]{2,1,0:T(2,128)(2,1)S(1)} async-done(((bf16[32,2,2048]{2,1,0:T(2,128)(2,1)}), bf16[32,2,2048]{2,1,0:T(2,128)(2,1)S(1)}, u32[]{:S(2)}, u32[]{:S(2)}) %all-to-all-start.3) | async-done | bytes 262176 | tf_op jit(solution)/shard_map/all_to_all | solution.py:87
  83.5 2.2 %reduce.21 = bf16[32,4096]{1,0:T(8,128)(2,1)S(1)} reduce(bf16[32,1,4096]{2,1,0:T(2,128)(2,1)S(1)} %broadcast_in_dim.61, bf16[]{:T(256)} %broadcast.448), dimensions={1}, to_apply=%broadcast_in_dim.61.reduce_sub_computation | reduce | bytes 524290 | tf_op jit(solution)/shard_map/broadcast_in_dim | solution.py:24
  86.5 5.7 %all-to-all-start.4 = ((bf16[32,2,2048]{2,1,0:T(2,128)(2,1)}), bf16[32,2,2048]{2,1,0:T(2,128)(2,1)S(1)}, u32[]{:S(2)}, u32[]{:S(2)}) async-start(bf16[32,2,2048]{2,1,0:T(2,128)(2,1)} %reshape.714), calls=%async_computation.4 | async-start | bytes 524288 | tf_op jit(solution)/shard_map/all_to_all | solution.py:23
  92.4 7.2 %all-to-all-done.4 = bf16[32,2,2048]{2,1,0:T(2,128)(2,1)S(1)} async-done(((bf16[32,2,2048]{2,1,0:T(2,128)(2,1)}), bf16[32,2,2048]{2,1,0:T(2,128)(2,1)S(1)}, u32[]{:S(2)}, u32[]{:S(2)}) %all-to-all-start.4) | async-done | bytes 262176 | tf_op jit(solution)/shard_map/all_to_all | solution.py:23
  102.0 32.3 %all_to_all.40 = bf16[8,1,16,4096]{3,2,1,0:T(8,128)(2,1)S(1)} all-to-all(bf16[8,1,16,4096]{3,2,1,0:T(8,128)(2,1)S(1)} %broadcast_in_dim.64), channel_id=1, replica_groups=mesh['dp'=8,'expert'=8,'mp'=4] {'dp'}, dimensions={0} | all-to-all | bytes 2097152 | tf_op jit(solution)/shard_map/all_to_all | solution.py:23
  134.7 1.1 copy-done.4
  136.8 1.2 convert_element_type.258
  138.0 4.9 %all-to-all-start.6 = ((bf16[32,4,4096]{2,1,0:T(4,128)(2,1)}), bf16[32,4,4096]{2,1,0:T(4,128)(2,1)S(1)}, u32[]{:S(2)}, u32[]{:S(2)}) async-start(bf16[32,4,4096]{2,1,0:T(4,128)(2,1)} %convert_element_type.258), calls=%async_computation.6 | async-start | bytes 2097152 | tf_op jit(solution)/shard_map/all_to_all | solution.py:87
  143.2 27.8 %all-to-all-done.6 = bf16[32,4,4096]{2,1,0:T(4,128)(2,1)S(1)} async-done(((bf16[32,4,4096]{2,1,0:T(4,128)(2,1)}), bf16[32,4,4096]{2,1,0:T(4,128)(2,1)S(1)}, u32[]{:S(2)}, u32[]{:S(2)}) %all-to-all-start.6) | async-done | bytes 1048608 | tf_op jit(solution)/shard_map/all_to_all | solution.py:87
  173.7 6.3 %all-to-all-start.7 = ((bf16[32,2,2048]{2,1,0:T(2,128)(2,1)}), bf16[32,2,2048]{2,1,0:T(2,128)(2,1)S(1)}, u32[]{:S(2)}, u32[]{:S(2)}) async-start(bf16[32,2,2048]{2,1,0:T(2,128)(2,1)} %reshape.716), calls=%async_computation.7 | async-start | bytes 524288 | tf_op jit(solution)/shard_map/all_to_all | solution.py:87
  180.0 7.2 %all-to-all-done.7 = bf16[32,2,2048]{2,1,0:T(2,128)(2,1)S(1)} async-done(((bf16[32,2,2048]{2,1,0:T(2,128)(2,1)}), bf16[32,2,2048]{2,1,0:T(2,128)(2,1)S(1)}, u32[]{:S(2)}, u32[]{:S(2)}) %all-to-all-start.7) | async-done | bytes 262176 | tf_op jit(solution)/shard_map/all_to_all | solution.py:87
  188.0 1.5 add_convert_fusion.1
  (136 shorter events, 23.8 us)
Async XLA Ops:
  0.0 136.3 %copy-start = (bf16[1,256,4096]{2,1,0:T(8,128)(2,1)S(1)}, bf16[1,256,4096]{2,1,0:T(8,128)(2,1)}, u32[]{:S(2)}) copy-start(bf16[1,256,4096]{2,1,0:T(8,128)(2,1)} %param.27) | copy-start | bytes 6291460
  0.0 14.3 %copy-start.1 = (s32[256]{0:T(256)S(1)}, s32[256]{0:T(256)}, u32[]{:S(2)}) copy-start(s32[256]{0:T(256)} %param.17) | copy-start | bytes 3076
  1.7 13.4 %copy-start.7 = (bf16[32,512]{1,0:T(8,128)(2,1)S(1)}, bf16[32,512]{1,0:T(8,128)(2,1)}, u32[]{:S(2)}) copy-start(bf16[32,512]{1,0:T(8,128)(2,1)} %param.14) | copy-start | bytes 98308
  1.7 23.5 %all-to-all-start = ((bf16[8,32,512]{2,1,0:T(8,128)(2,1)}), bf16[8,32,512]{2,1,0:T(8,128)(2,1)S(1)}, u32[]{:S(2)}, u32[]{:S(2)}) async-start(bf16[8,32,512]{2,1,0:T(8,128)(2,1)} %broadcast_in_dim.55), calls=%async_computation | async-start | bytes 524288 | tf_op jit(solution)/shard_map/all_to_all | solution.py:23
  20.4 4.6 %copy-start.9 = (bf16[2,32,128]{2,1,0:T(8,128)(2,1)S(1)}, bf16[2,32,128]{2,1,0:T(8,128)(2,1)}, u32[]{:S(2)}) copy-start(bf16[2,32,128]{2,1,0:T(8,128)(2,1)} %param.15) | copy-start | bytes 49156
  32.2 19.1 %all-to-all-start.1 = ((bf16[1,32,4,130]{3,2,0,1:T(4,128)(2,1)}), bf16[1,32,4,130]{3,2,0,1:T(4,128)(2,1)S(1)}, u32[]{:S(2)}, u32[]{:S(2)}) async-start(bf16[1,32,4,130]{3,2,0,1:T(4,128)(2,1)} %maximum_bitcast_fusion), calls=%async_computation.1 | async-start | bytes 131072 | tf_op jit(solution)/shard_map/all_to_all | solution.py:37
  42.6 23.4 %copy-start.5 = (bf16[128,4096]{1,0:T(8,128)(2,1)S(1)}, bf16[128,4096]{1,0:T(8,128)(2,1)}, u32[]{:S(2)}) copy-start(bf16[128,4096]{1,0:T(8,128)(2,1)} %param.22) | copy-start | bytes 3145732
  55.0 9.4 %all-to-all-start.2 = ((bf16[4,130,128]{2,1,0:T(8,128)(2,1)}), bf16[4,130,128]{2,1,0:T(8,128)(2,1)S(1)}, u32[]{:S(2)}, u32[]{:S(2)}) async-start(bf16[4,130,128]{2,1,0:T(8,128)(2,1)} %broadcast_in_dim.60), calls=%async_computation.2 | async-start | bytes 278528 | tf_op jit(solution)/shard_map/all_to_all | solution.py:23
  65.5 9.5 %copy-start.10 = (s32[256,2]{0,1:T(2,128)S(1)}, s32[256,2]{0,1:T(2,128)}, u32[]{:S(2)}) copy-start(s32[256,2]{0,1:T(2,128)} %param.23) | copy-start | bytes 6148
  68.5 13.8 %all-to-all-start.3 = ((bf16[32,2,2048]{2,1,0:T(2,128)(2,1)}), bf16[32,2,2048]{2,1,0:T(2,128)(2,1)S(1)}, u32[]{:S(2)}, u32[]{:S(2)}) async-start(bf16[32,2,2048]{2,1,0:T(2,128)(2,1)} %reshape.712), calls=%async_computation.3 | async-start | bytes 524288 | tf_op jit(solution)/shard_map/all_to_all | solution.py:87
  83.0 17.4 %copy-start.6 = (bf16[32,4096]{1,0:T(8,128)(2,1)S(1)}, bf16[32,4096]{1,0:T(8,128)(2,1)}, u32[]{:S(2)}) copy-start(bf16[32,4096]{1,0:T(8,128)(2,1)} %param.20) | copy-start | bytes 786436
  85.7 16.0 %copy-start.8 = (f32[4096]{0:T(1024)S(1)}, f32[4096]{0:T(1024)}, u32[]{:S(2)}) copy-start(f32[4096]{0:T(1024)} %param.21) | copy-start | bytes 49156
  86.5 13.0 %all-to-all-start.4 = ((bf16[32,2,2048]{2,1,0:T(2,128)(2,1)}), bf16[32,2,2048]{2,1,0:T(2,128)(2,1)S(1)}, u32[]{:S(2)}, u32[]{:S(2)}) async-start(bf16[32,2,2048]{2,1,0:T(2,128)(2,1)} %reshape.714), calls=%async_computation.4 | async-start | bytes 524288 | tf_op jit(solution)/shard_map/all_to_all | solution.py:23
  100.8 0.8 copy-start.2
  100.8 33.5 %copy-start.3 = (bf16[1,4096,256]{2,1,0:T(8,128)(2,1)S(1)}, bf16[1,4096,256]{2,1,0:T(8,128)(2,1)}, u32[]{:S(2)}) copy-start(bf16[1,4096,256]{2,1,0:T(8,128)(2,1)} %param.25) | copy-start | bytes 6291460
  134.3 1.6 copy-start.4
  136.8 6.2 %copy-start.11 = (f32[256,2]{0,1:T(2,128)S(1)}, f32[256,2]{0,1:T(2,128)}, u32[]{:S(2)}) copy-start(f32[256,2]{0,1:T(2,128)} %param.24) | copy-start | bytes 6148
  138.0 32.9 %all-to-all-start.6 = ((bf16[32,4,4096]{2,1,0:T(4,128)(2,1)}), bf16[32,4,4096]{2,1,0:T(4,128)(2,1)S(1)}, u32[]{:S(2)}, u32[]{:S(2)}) async-start(bf16[32,4,4096]{2,1,0:T(4,128)(2,1)} %convert_element_type.258), calls=%async_computation.6 | async-start | bytes 2097152 | tf_op jit(solution)/shard_map/all_to_all | solution.py:87
  173.7 13.6 %all-to-all-start.7 = ((bf16[32,2,2048]{2,1,0:T(2,128)(2,1)}), bf16[32,2,2048]{2,1,0:T(2,128)(2,1)S(1)}, u32[]{:S(2)}, u32[]{:S(2)}) async-start(bf16[32,2,2048]{2,1,0:T(2,128)(2,1)} %reshape.716), calls=%async_computation.7 | async-start | bytes 524288 | tf_op jit(solution)/shard_map/all_to_all | solution.py:87
where the time goes:
time: 193 us; the launch traced here: 190 us
  waiting for transfers between devices  62.2 us (32%)
  starting transfers between devices  47.3 us (25%)
  blocking collectives  32.3 us (17%)
  local copies, waits for them, and re-layouts  29.2 us (15%)
  other arithmetic  10.5 us (5%)
  matrix products  7.56 us (4%)
    all_to_all x3, waiting for transfers between devices, summed_on_arrival(): lax.all_to_all(parts, axis, split_axis=0, concat_axis=0, tiled=True)  41.8 us
    all_to_all x1, blocking collectives, from_everyone(): lax.all_to_all(jnp.broadcast_to(array[None], (count, *array.shape)), axis...  32.3 us
    all_to_all x3, starting transfers between devices, from_everyone(): lax.all_to_all(jnp.broadcast_to(array[None], (count, *array.shape)), axis...  19.1 us
    all_to_all x3, starting transfers between devices, summed_on_arrival(): lax.all_to_all(parts, axis, split_axis=0, concat_axis=0, tiled=True)  17.8 us
    all_to_all x3, waiting for transfers between devices, from_everyone(): lax.all_to_all(jnp.broadcast_to(array[None], (count, *array.shape)), axis...  11.7 us
    all_to_all x1, starting transfers between devices, in_one_piece(): lax.all_to_all(both, axis, split_axis=split_dim, concat_axis=concat_dim,...  10.4 us
    gather x2, local copies, waits for them, and re-layouts, body(): page_contents = page_cache[:, pick_slot]  9.87 us
    all_to_all x1, waiting for transfers between devices, in_one_piece(): lax.all_to_all(both, axis, split_axis=split_dim, concat_axis=concat_dim,...  8.67 us
  transfers between devices with their start and end apart: 7, of which 6 were waited for; matrix products, arithmetic and copies ran while one was open for 8% of the time, Pallas kernels for 0%

commit v1 on v0

v1 whole, which is shorter than its diff:
```python
import functools

import jax
import jax.numpy as jnp
from jax import lax
from jax.experimental import pallas as pl
from jax.experimental.pallas import tpu as pltpu
from jax.sharding import Mesh, PartitionSpec as P

bf16 = jnp.bfloat16
f32 = jnp.float32
i32 = jnp.int32

DP, NX, NC, MP = 8, 4, 2, 4
EXPERTS = NX * NC
HOLDERS = DP * MP
PMAX = 4
SEQ = 32
TOTAL = DP * SEQ
SLOTS = 32
PAGE = 256
HEAD = 128
GROUPS = 4
D = 4096
FF = 256
CHIPS = NX * MP
COLS = D // CHIPS
HALF = SEQ // NC
ROWS = DP * HALF
FLOOR = -1e30
SCALE = HEAD ** (-0.5)


def iota(shape, dim):
    return lax.broadcasted_iota(i32, shape, dim)


def dot(a, b, dims=((1,), (0,))):
    return lax.dot_general(a, b, (dims, ((), ())), preferred_element_type=f32)


def one_hot(mask):
    return jnp.where(mask, 1.0, 0.0).astype(bf16)


def core_rows(core, count):
    row = iota((count, SEQ), 0)
    wanted = (row // MP) * (NC * MP) + core * MP + row % MP
    return one_hot(wanted == iota((count, SEQ), 1))


def select_kernel(place, queries, holders, out):
    lane = iota((GROUPS * SEQ, HEAD), 1)
    sub = iota((GROUPS * SEQ, HEAD), 0)
    table = jnp.concatenate([holders[...]] * GROUPS, axis=0)
    named = jnp.zeros((GROUPS * SEQ, HEAD), i32)
    for j in range(PMAX):
        named = jnp.where(lane % PMAX == j, table[:, j : j + 1], named)
    wanted = (lane // (GROUPS * PMAX)) * MP + place[3]
    same_head = (lane // PMAX) % GROUPS == sub // SEQ
    pick = one_hot((named == wanted) & same_head)
    stacked = jnp.concatenate(
        [queries[:, k * HEAD : (k + 1) * HEAD] for k in range(GROUPS)], axis=0
    )
    out[...] = dot(pick, stacked, ((0,), (0,))).astype(bf16)


def index_kernel(place, holders, slots, lengths, spread, live, gather):
    lane = iota((TOTAL, HEAD), 1)
    sub = iota((TOTAL, HEAD), 0)
    mine = place[0] * MP + place[3]
    named = jnp.zeros((TOTAL, HEAD), i32)
    slot = jnp.zeros((TOTAL, HEAD), i32)
    for j in range(PMAX):
        here = lane % PMAX == j
        named = jnp.where(here, holders[:, j : j + 1], named)
        slot = jnp.where(here, slots[:, j : j + 1], slot)
    keep = (named == mine) & (sub // SEQ == lane // (GROUPS * PMAX))
    slot_row = jnp.sum(jnp.where(keep, slot, 0), axis=0, keepdims=True)
    length_row = jnp.sum(jnp.where(keep, lengths[...], 0), axis=0, keepdims=True)
    one_lane = lane[0:1]
    live_row = jnp.clip(length_row - PAGE * (one_lane % PMAX), 0, PAGE)
    head_lane = (lane // PMAX) % GROUPS
    match = (slot_row == sub // 8) & (head_lane == sub % GROUPS)
    spread[...] = one_hot(match)
    count = jnp.sum(jnp.where(match, live_row, 0), axis=1, keepdims=True)
    live[...] = jnp.broadcast_to(count, (TOTAL, HEAD))
    own = (lane // (GROUPS * PMAX) == sub // SEQ) & (head_lane == (sub // 8) % GROUPS)
    own = own & (lane % PMAX == sub % PMAX)
    target = jnp.sum(jnp.where(own, slot_row, 0), axis=1, keepdims=True)
    rows = iota((TOTAL, 1), 0)
    target = target * 8 + (rows // 8) % GROUPS + jnp.where(rows % 8 < PMAX, 0, TOTAL)
    gather[...] = one_hot(target == iota((TOTAL, 2 * TOTAL), 1))


STEP = 8


def attend_kernel(queries, spread, live, gather, pages, out, parts):
    step = pl.program_id(0)
    wanted = dot(spread[...], queries[...])
    scores = jnp.concatenate(
        [
            dot(wanted[k * 8 : (k + 1) * 8].astype(bf16), pages[0, k, 0], ((1,), (1,)))
            for k in range(STEP)
        ],
        axis=0,
    )
    scores = scores * SCALE
    is_live = iota((STEP * 8, PAGE), 1) < live[:, 0:1]
    masked = jnp.where(is_live, scores, FLOOR)
    top = jnp.max(masked, axis=1, keepdims=True).astype(bf16).astype(f32)
    weights = jnp.where(is_live, jnp.exp(masked - top), 0.0)
    total = jnp.sum(weights, axis=1, keepdims=True)
    coarse = weights.astype(bf16).astype(f32)
    first = iota((STEP * 8, PAGE), 0) % 8 < GROUPS
    split = jnp.where(first, coarse, weights - coarse)
    found = []
    for k in range(STEP):
        both = dot(split[k * 8 : (k + 1) * 8].astype(bf16), pages[0, k, 1])
        found.append(both + pltpu.roll(both, GROUPS, 0))
    start = pl.multiple_of(step * (STEP * 8), STEP * 8)
    parts[pl.ds(start, STEP * 8), :] = jnp.concatenate(found, axis=0)
    lane = iota((STEP * 8, HEAD), 1)
    high = total.astype(bf16).astype(f32)
    tops = jnp.where(lane < 64, top, jnp.where(lane < 96, high, total - high))
    parts[pl.ds(TOTAL + start, STEP * 8), :] = tops

    @pl.when(step == SLOTS // STEP - 1)
    def _():
        out[...] = dot(gather[...], parts[...].astype(bf16)).astype(bf16)


PROJ = 4


def project_kernel(
    place, received, queries, fresh, holders, weight, mine, theirs, attended
):
    step = pl.program_id(0)

    @pl.when(step == 0)
    def _():
        table = holders[...]
        lane = iota((SEQ, TOTAL), 1)
        order = jnp.concatenate(
            [one_hot(table[:, r % PMAX : r % PMAX + 1] * 8 + r == lane) for r in range(8)],
            axis=0,
        )
        sorted_parts = dot(order, received[...])
        pages = [sorted_parts[j * SEQ : (j + 1) * SEQ] for j in range(PMAX)]
        scalars = [sorted_parts[(PMAX + j) * SEQ : (PMAX + j + 1) * SEQ] for j in range(PMAX)]
        own = (
            jnp.sum(
                queries[...].astype(f32) * fresh[0].astype(f32), axis=1, keepdims=True
            )
            * SCALE
        )
        highest = own
        for part in scalars:
            highest = jnp.maximum(highest, part[:, 0:1])
        factor = jnp.exp(own - highest)
        total = factor
        weighted = factor * fresh[1].astype(f32)
        for page, part in zip(pages, scalars):
            factor = jnp.exp(part[:, 0:1] - highest)
            total = total + (part[:, 64:65] + part[:, 96:97]) * factor
            weighted = weighted + page * factor
        rows = (weighted / total).astype(bf16)
        order = jnp.concatenate(
            [core_rows(place[2], HALF), core_rows(1 - place[2], HALF)], axis=0
        )
        attended[...] = dot(order, rows).astype(bf16)

    result = dot(attended[...], weight[...])
    for k in range(CHIPS // PROJ):
        block = result[:, k * COLS : (k + 1) * COLS]
        mine[k] = block[:HALF]
        theirs[k] = block[HALF:].astype(bf16)


def residual_kernel(place, received, tokens, gain, out):
    summed = jnp.sum(received[...].astype(f32), axis=0)
    own = dot(core_rows(place[2], HALF), tokens[...])
    gained = ((summed + own) * gain[...]).astype(bf16)
    out[...] = jnp.broadcast_to(gained[None], (DP, HALF, COLS))


def spread_kernel(rows, out):
    out[...] = jnp.broadcast_to(rows[...][None], out.shape)


UNITS = 4
BLOCKS = CHIPS // UNITS


def hidden_kernel(rows, gain, gate, up, routed, out, gate_sum, up_sum, squares):
    step = pl.program_id(0)

    @pl.when(step == 0)
    def _():
        gate_sum[...] = jnp.zeros_like(gate_sum)
        up_sum[...] = jnp.zeros_like(up_sum)
        squares[...] = jnp.zeros_like(squares)

    for k in range(BLOCKS):
        part = rows[k]
        weights = slice(k * COLS, (k + 1) * COLS)
        gate_sum[...] += dot(part, gate[0, weights])
        up_sum[...] += dot(part, up[0, weights])
        plain = part.astype(f32) / gain[:, weights]
        squares[...] += plain * plain

    @pl.when(step == UNITS - 1)
    def _():
        mean = jnp.sum(squares[...], axis=1, keepdims=True) * (1.0 / D)
        scale = lax.rsqrt(mean + 1e-05)
        gated = gate_sum[...] * scale
        value = gated / (1.0 + jnp.exp(-gated)) * (up_sum[...] * scale)
        value = (value * routed[...]).astype(bf16)
        row = iota((ROWS, ROWS), 0)
        order = one_hot((row % DP) * CHIPS + row // DP == iota((ROWS, ROWS), 1))
        out[...] = dot(order, value).astype(bf16)


def down_kernel(hidden, weight, out):
    out[...] = dot(hidden[...], weight[0]).astype(bf16)


def chip_sum_kernel(received, out):
    summed = jnp.sum(received[...].astype(f32), axis=0)
    out[...] = summed.reshape(DP, out.shape[1], HEAD).astype(bf16)


def final_kernel(received, residual, out):
    summed = jnp.sum(received[...].astype(f32), axis=0) + residual[...]
    for k in range(D // HEAD):
        out[:, k * HEAD : (k + 1) * HEAD] = summed[k : k + 1].astype(bf16)


def call(kernel, out_shape, grid, in_specs, out_specs, scratch=(), place=False, name=None):
    return pl.pallas_call(
        kernel,
        out_shape=out_shape,
        grid_spec=pltpu.PrefetchScalarGridSpec(
            num_scalar_prefetch=1 if place else 0,
            grid=grid,
            in_specs=in_specs,
            out_specs=out_specs,
            scratch_shapes=scratch,
        ),
        compiler_params=pltpu.CompilerParams(
            dimension_semantics=("arbitrary",) * len(grid)
        ),
        name=name,
    )


def whole(shape):
    return pl.BlockSpec(shape, lambda *_: (0,) * len(shape))


def struct(shape, dtype=bf16):
    return jax.ShapeDtypeStruct(shape, dtype)


def exchange(array, axes):
    return lax.all_to_all(array, axes, 0, 0, tiled=True)


def swap(array):
    return lax.ppermute(array, "core", [(0, 1), (1, 0)])


def body(
    queries,
    fresh_entries,
    page_cache,
    lengths,
    page_holder,
    page_slot,
    tokens,
    norm_gain,
    out_weight,
    expert_ids,
    gate_values,
    gate_weight,
    up_weight,
    down_weight,
):
    dp, x, core, mp = (lax.axis_index(n) for n in ("dp", "x", "core", "mp"))
    place = jnp.stack([dp, x, core, mp]).astype(i32)
    gain = norm_gain.reshape(1, D)

    selected = call(
        select_kernel,
        struct((DP * GROUPS * PMAX, HEAD)),
        (1,),
        [
            whole((SEQ, GROUPS * HEAD)),
            pl.BlockSpec((SEQ, PMAX), lambda _, p: (p[0], 0)),
        ],
        whole((DP * GROUPS * PMAX, HEAD)),
        place=True,
        name="select",
    )(place, queries, page_holder)
    asked = exchange(selected.reshape(DP, GROUPS * PMAX, HEAD), "dp")
    asked = asked.reshape(DP * GROUPS * PMAX, HEAD)

    spread, live, gather = call(
        index_kernel,
        (struct((TOTAL, HEAD)), struct((TOTAL, HEAD), i32), struct((TOTAL, 2 * TOTAL))),
        (1,),
        [whole((TOTAL, PMAX)), whole((TOTAL, PMAX)), whole((TOTAL, 1))],
        (whole((TOTAL, HEAD)), whole((TOTAL, HEAD)), whole((TOTAL, 2 * TOTAL))),
        place=True,
        name="index",
    )(place, page_holder, page_slot, lengths.reshape(TOTAL, 1))

    parts = call(
        attend_kernel,
        struct((TOTAL, HEAD)),
        (SLOTS // STEP,),
        [
            whole((DP * GROUPS * PMAX, HEAD)),
            pl.BlockSpec((STEP * 8, HEAD), lambda s: (s, 0)),
            pl.BlockSpec((STEP * 8, HEAD), lambda s: (s, 0)),
            whole((TOTAL, 2 * TOTAL)),
            pl.BlockSpec((1, STEP, 2, PAGE, HEAD), lambda s: (0, s, 0, 0, 0)),
        ],
        whole((TOTAL, HEAD)),
        scratch=[pltpu.VMEM((2 * TOTAL, HEAD), f32)],
        name="attend",
    )(asked, spread, live, gather, page_cache)
    parts = exchange(parts.reshape(HOLDERS, 8, HEAD), ("dp", "mp"))
    parts = parts.reshape(TOTAL, HEAD)

    mine, theirs = call(
        project_kernel,
        (struct((CHIPS, HALF, COLS), f32), struct((CHIPS, HALF, COLS))),
        (PROJ,),
        [
            whole((TOTAL, HEAD)),
            pl.BlockSpec((SEQ, HEAD), lambda _, p: (0, p[3])),
            whole((2, SEQ, HEAD)),
            pl.BlockSpec((SEQ, PMAX), lambda _, p: (p[0], 0)),
            pl.BlockSpec((HEAD, D // PROJ), lambda s, _: (0, s)),
        ],
        (
            pl.BlockSpec((CHIPS // PROJ, HALF, COLS), lambda s, _: (s, 0, 0)),
            pl.BlockSpec((CHIPS // PROJ, HALF, COLS), lambda s, _: (s, 0, 0)),
        ),
        scratch=[pltpu.VMEM((SEQ, HEAD), bf16)],
        place=True,
        name="project",
    )(place, parts, queries, fresh_entries, page_holder, out_weight)
    joined = (mine + swap(theirs).astype(f32)).astype(bf16)
    joined = exchange(joined, ("x", "mp"))

    gained = call(
        residual_kernel,
        struct((DP, HALF, COLS)),
        (1,),
        [
            whole((CHIPS, HALF, COLS)),
            pl.BlockSpec((SEQ, COLS), lambda _, p: (0, p[1] * MP + p[3])),
            pl.BlockSpec((1, COLS), lambda _, p: (0, p[1] * MP + p[3])),
        ],
        whole((DP, HALF, COLS)),
        place=True,
        name="residual",
    )(place, joined, tokens, gain)
    gained = exchange(gained, "dp").reshape(ROWS, COLS)
    copies = call(
        spread_kernel,
        struct((CHIPS, ROWS, COLS)),
        (1,),
        [whole((ROWS, COLS))],
        whole((CHIPS, ROWS, COLS)),
        name="spread",
    )(gained)
    own_rows = exchange(copies, ("x", "mp"))
    other_rows = swap(own_rows)

    expert = x * NC + core
    routed = jnp.sum(jnp.where(expert_ids == expert, gate_values, 0.0), axis=1)
    routed = routed.reshape(DP, NX, NC, MP).transpose(2, 0, 1, 3).reshape(NC, ROWS, 1)
    own_routed = lax.dynamic_index_in_dim(routed, core, 0, keepdims=False)
    other_routed = lax.dynamic_index_in_dim(routed, 1 - core, 0, keepdims=False)

    hidden = call(
        hidden_kernel,
        struct((ROWS, FF)),
        (UNITS,),
        [
            pl.BlockSpec((BLOCKS, ROWS, COLS), lambda s: (s, 0, 0)),
            pl.BlockSpec((1, D // UNITS), lambda s: (0, s)),
            pl.BlockSpec((1, D // UNITS, FF), lambda s: (0, s, 0)),
            pl.BlockSpec((1, D // UNITS, FF), lambda s: (0, s, 0)),
            whole((ROWS, 1)),
        ],
        whole((ROWS, FF)),
        scratch=[pltpu.VMEM((ROWS, FF), f32) for _ in range(3)],
        name="hidden",
    )
    down = call(
        down_kernel,
        struct((ROWS, D)),
        (4,),
        [whole((ROWS, FF)), pl.BlockSpec((1, FF, D // 4), lambda s: (0, 0, s))],
        pl.BlockSpec((ROWS, D // 4), lambda s: (0, s)),
        name="down",
    )
    own_hidden = hidden(own_rows, gain, gate_weight, up_weight, own_routed)
    other_hidden = hidden(other_rows, gain, gate_weight, up_weight, other_routed)
    other_out = down(other_hidden, down_weight)
    passed = swap(other_out)
    own_out = down(own_hidden, down_weight)
    summed = (own_out.astype(f32) + passed.astype(f32)).astype(bf16)
    summed = exchange(summed.reshape(CHIPS, DP, D), ("x", "mp"))
    rows = call(
        chip_sum_kernel,
        struct((DP, D // HEAD, HEAD)),
        (2,),
        [pl.BlockSpec((CHIPS, DP, D // 2), lambda s: (0, 0, s))],
        pl.BlockSpec((DP, D // HEAD // 2, HEAD), lambda s: (0, s, 0)),
        name="chip_sum",
    )(summed)
    rows = exchange(rows, "dp")

    home = dp * CHIPS + x * MP + mp
    residual = lax.dynamic_slice_in_dim(own_rows, home, 1, 1).reshape(1, D).astype(f32) / gain
    return call(
        final_kernel,
        struct((1, D)),
        (1,),
        [whole((DP, D // HEAD, HEAD)), whole((D // HEAD, HEAD))],
        whole((1, D)),
        name="final",
    )(rows, residual.reshape(D // HEAD, HEAD))


def solution(mesh):
    fine = Mesh(mesh.devices.reshape(DP, NX, NC, MP), ("dp", "x", "core", "mp"))
    expert = ("x", "core")
    return jax.shard_map(
        body,
        mesh=fine,
        in_specs=(
            P("dp", expert),
            P(None, "dp", expert),
            P(expert, ("dp", "mp"), None, None, None),
            P(),
            P(),
            P(),
            P("dp", None),
            P(),
            P((*expert, "mp"), None),
            P(),
            P(),
            P(expert, None, ("dp", "mp")),
            P(expert, None, ("dp", "mp")),
            P(expert, ("dp", "mp"), None),
        ),
        out_specs=P(("dp", *expert, "mp"), None),
        check_vma=False,
    )
```

time: 193 us -> 165 us (0.85)
  Pallas kernels: 0 us -> 40.5 us
  waiting for transfers between devices: 62.2 us -> 29.3 us
  starting transfers between devices: 47.3 us -> 17 us
  blocking collectives: 32.3 us -> 61.5 us
  local copies, waits for them, and re-layouts: 29.2 us -> 9.37 us
  matrix products: 7.56 us -> 0 us
  other arithmetic: 10.5 us -> 5.6 us
    pallas_call x0 -> x12, Pallas kernels: none -> 40.5 us  [the longest x1 5.19 us: body(): call(attend_kernel, struct((TOTAL, HEAD)), (SLOTS // STEP,), [whole((DP *...]
    all_to_all x7 -> x3, waiting for transfers between devices: 62.2 us -> 26.2 us  [exchange(): return lax.all_to_all(array, axes, 0, 0, tiled=True)]
    all_to_all x7 -> x3, starting transfers between devices: 47.3 us -> 16.8 us  [exchange(): return lax.all_to_all(array, axes, 0, 0, tiled=True)]
    all_to_all x1 -> x4, blocking collectives: 32.3 us -> 61.5 us  [exchange(): return lax.all_to_all(array, axes, 0, 0, tiled=True)]
    gather x7 -> x0, local copies, waits for them, and re-layouts: 13 us -> none  [the longest x2 9.87 us: body(): page_contents = page_cache[:, pick_slot]]
    dot_general x9 -> x0, matrix products: 7.56 us -> none  [the longest x1 2.58 us: body(): jnp.einsum('kngt,kntd->kngd', weights, page_contents[:, :, 1].astype(jnp....]
    ppermute x0 -> x3, waiting for transfers between devices: none -> 3.17 us  [swap(): return lax.ppermute(array, 'core', [(0, 1), (1, 0)])]
    broadcast_in_dim x4 -> x0, local copies, waits for them, and re-layouts: 2.88 us -> none  [from_everyone(): jnp.broadcast_to(array[None], (count, *array.shape))]
  transfers between devices with their start and end apart: 7 -> 6, of which waited for: 6 -> 5; matrix products, arithmetic and copies ran while one was open for 8% -> 4% of each run, Pallas kernels for 0% -> 7%
where the time goes in v1:
time: 165 us; the launch traced here: 163 us
  blocking collectives  61.5 us (37%)
  Pallas kernels  40.5 us (25%)
  waiting for transfers between devices  29.3 us (18%)
  starting transfers between devices  17 us (10%)
  local copies, waits for them, and re-layouts  9.37 us (6%)
  other arithmetic  5.6 us (3%)
    all_to_all x4, blocking collectives, exchange(): return lax.all_to_all(array, axes, 0, 0, tiled=True)  61.5 us
    all_to_all x3, waiting for transfers between devices, exchange(): return lax.all_to_all(array, axes, 0, 0, tiled=True)  26.2 us
    all_to_all x3, starting transfers between devices, exchange(): return lax.all_to_all(array, axes, 0, 0, tiled=True)  16.8 us
    unnamed x18, local copies, waits for them, and re-layouts  6.19 us
    pallas_call x1, Pallas kernels, body(): call(attend_kernel, struct((TOTAL, HEAD)), (SLOTS // STEP,), [whole((DP *...  5.19 us
    pallas_call x1, Pallas kernels, body(): call(project_kernel, (struct((CHIPS, HALF, COLS), f32), struct((CHIPS, HA...  4.8 us
    pallas_call x1, Pallas kernels, body(): own_hidden = hidden(own_rows, gain, gate_weight, up_weight, own_routed)  4.73 us
    pallas_call x1, Pallas kernels, body(): hidden(other_rows, gain, gate_weight, up_weight, other_routed)  4.69 us
  transfers between devices with their start and end apart: 6, of which 5 were waited for; matrix products, arithmetic and copies ran while one was open for 4% of the time, Pallas kernels for 7%

profile of v1, /device:TPU:8, one launch (start us, length us, event | category | flops | bytes accessed | tf_op | source)
XLA Modules:
  0.0 163.4 jit_solution(11234808287633018017)
XLA Ops:
  2.1 2.3 %select.1 = bf16[128,128]{1,0:T(8,128)(2,1)} custom-call(s32[4]{0:T(128)} %pad_add_fusion.place, bf16[32,512]{1,0:T(8,128)(2,1)} %queries.3, s32[256,4]{1,0:T(8,128)} %copy.21.holders), custom_call_target="tpu_custom_call" | custom-call | tf_op jit(solution)/shard_map/select/pallas_call | solution.py:295
  4.4 8.5 %all-to-all-start = ((bf16[8,16,128]{2,1,0:T(8,128)(2,1)}), bf16[8,16,128]{2,1,0:T(8,128)(2,1)S(1)}, u32[]{:S(2)}, u32[]{:S(2)}) async-start(bf16[8,16,128]{2,1,0:T(8,128)(2,1)} %bitcast.29), calls=%async_computation | async-start | bytes 65536 | tf_op jit(solution)/shard_map/all_to_all | solution.py:268
  15.8 3.1 %index.1 = (bf16[256,128]{1,0:T(8,128)(2,1)}, s32[256,128]{1,0:T(8,128)}, bf16[256,512]{1,0:T(8,128)(2,1)}) custom-call(s32[4]{0:T(128)} %pad_add_fusion.place, s32[256,4]{1,0:T(8,128)} %copy.21.holders, s32[256,4]{1,0:T(8,128)} %copy.23.slots, s32[256,1]{1,0:T(8,128)} %copy.24.lengths), custom_call_target="tpu_custom_call" | custom-call | tf_op jit(solution)/shard_map/index/pallas_call | solution.py:310
  18.9 2.0 %all-to-all-done = bf16[8,16,128]{2,1,0:T(8,128)(2,1)S(1)} async-done(((bf16[8,16,128]{2,1,0:T(8,128)(2,1)}), bf16[8,16,128]{2,1,0:T(8,128)(2,1)S(1)}, u32[]{:S(2)}, u32[]{:S(2)}) %all-to-all-start) | async-done | bytes 32800 | tf_op jit(solution)/shard_map/all_to_all | solution.py:268
  21.5 5.2 %attend.1 = bf16[256,128]{1,0:T(8,128)(2,1)} custom-call(bf16[128,128]{1,0:T(8,128)(2,1)} %bitcast.27, bf16[256,128]{1,0:T(8,128)(2,1)} %get-tuple-element.10.spread, s32[256,128]{1,0:T(8,128)} %get-tuple-element.11.live, bf16[256,512]{1,0:T(8,128)(2,1)} %get-tuple-element.12.gather, bf16[1,32,2,256,128]{4,3,2,1,0:T(8,128)(2,1)} %pages.1), custom_call_target="tpu_custom_call" | custom-call | tf_op jit(solution)/shard_map/attend/pallas_call | solution.py:320
  26.7 17.2 %all_to_all.35 = bf16[32,8,128]{2,1,0:T(8,128)(2,1)} all-to-all(bf16[32,8,128]{2,1,0:T(8,128)(2,1)} %bitcast.24), channel_id=1, replica_groups=mesh['dp'=8,'x'=4,'core'=2,'mp'=4] {'dp','mp'}, dimensions={0} | all-to-all | bytes 131072 | tf_op jit(solution)/shard_map/all_to_all | solution.py:268
  43.9 4.8 %project.1 = (f32[16,16,256]{2,1,0:T(8,128)}, bf16[16,16,256]{2,1,0:T(8,128)(2,1)}) custom-call(s32[4]{0:T(128)} %pad_add_fusion.place, bf16[256,128]{1,0:T(8,128)(2,1)} %bitcast.25, bf16[32,512]{1,0:T(8,128)(2,1)} %queries.3, bf16[2,32,128]{2,1,0:T(8,128)(2,1)} %fresh.1, s32[256,4]{1,0:T(8,128)} %copy.21.holders, bf16[128,4096]{1,0:T(8,128)(2,1)} %weight.3), custom_call_target="tpu_custom_call" | custom-call | tf_op jit(solution)/shard_map/project/pallas_call | solution.py:338
  48.8 1.6 collective-permute-done
  51.3 13.0 %all_to_all.36.received = bf16[16,16,256]{2,1,0:T(8,128)(2,1)} all-to-all(bf16[16,16,256]{2,1,0:T(8,128)(2,1)S(1)} %add_convert_fusion.1), channel_id=1, replica_groups=mesh['dp'=8,'x'=4,'core'=2,'mp'=4] {'x','mp'}, dimensions={0} | all-to-all | bytes 262144 | tf_op jit(solution)/shard_map/all_to_all | solution.py:268
  64.3 2.3 %residual.1 = bf16[8,16,256]{2,1,0:T(8,128)(2,1)} custom-call(s32[4]{0:T(128)} %pad_add_fusion.place, bf16[16,16,256]{2,1,0:T(8,128)(2,1)} %all_to_all.36.received, bf16[32,4096]{1,0:T(8,128)(2,1)} %tokens.1, f32[1,4096]{1,0:T(1,128)} %bitcast.21), custom_call_target="tpu_custom_call" | custom-call | tf_op jit(solution)/shard_map/residual/pallas_call | solution.py:360
  66.6 12.3 %all_to_all.37 = bf16[8,16,256]{2,1,0:T(8,128)(2,1)} all-to-all(bf16[8,16,256]{2,1,0:T(8,128)(2,1)} %residual.1), channel_id=1, replica_groups=mesh['dp'=8,'x'=4,'core'=2,'mp'=4] {'dp'}, dimensions={0} | all-to-all | bytes 131072 | tf_op jit(solution)/shard_map/all_to_all | solution.py:268
  79.0 1.9 %spread.1 = bf16[16,128,256]{2,1,0:T(8,128)(2,1)} custom-call(bf16[128,256]{1,0:T(8,128)(2,1)} %bitcast.26), custom_call_target="tpu_custom_call" | custom-call | tf_op jit(solution)/shard_map/spread/pallas_call | solution.py:374
  80.9 18.9 %all_to_all.38.rows = bf16[16,128,256]{2,1,0:T(8,128)(2,1)S(1)} all-to-all(bf16[16,128,256]{2,1,0:T(8,128)(2,1)} %spread.1), channel_id=1, replica_groups=mesh['dp'=8,'x'=4,'core'=2,'mp'=4] {'x','mp'}, dimensions={0} | all-to-all | bytes 2097152 | tf_op jit(solution)/shard_map/all_to_all | solution.py:268
  100.9 1.6 collective-permute-done.1.rows
  103.5 4.7 %hidden.3 = bf16[128,256]{1,0:T(8,128)(2,1)} custom-call(bf16[16,128,256]{2,1,0:T(8,128)(2,1)} %copy-done.2, f32[1,4096]{1,0:T(1,128)} %bitcast.22, bf16[1,4096,256]{2,1,0:T(8,128)(2,1)} %gate.3, bf16[1,4096,256]{2,1,0:T(8,128)(2,1)} %up.3, f32[128,1]{1,0:T(8,128)} %copy.28.routed), custom_call_target="tpu_custom_call" | custom-call | tf_op jit(solution)/shard_map/hidden/pallas_call | solution.py:415
  108.2 4.0 %down.3 = bf16[128,4096]{1,0:T(8,128)(2,1)} custom-call(bf16[128,256]{1,0:T(8,128)(2,1)} %hidden.3, bf16[1,256,4096]{2,1,0:T(8,128)(2,1)} %weight.5), custom_call_target="tpu_custom_call" | custom-call | tf_op jit(solution)/shard_map/down/pallas_call | solution.py:416
  113.1 4.7 %hidden.2 = bf16[128,256]{1,0:T(8,128)(2,1)} custom-call(bf16[16,128,256]{2,1,0:T(8,128)(2,1)} %copy-done, f32[1,4096]{1,0:T(1,128)} %bitcast.23, bf16[1,4096,256]{2,1,0:T(8,128)(2,1)} %gate.3, bf16[1,4096,256]{2,1,0:T(8,128)(2,1)} %up.3, f32[128,1]{1,0:T(8,128)} %copy.27.routed), custom_call_target="tpu_custom_call" | custom-call | tf_op jit(solution)/shard_map/hidden/pallas_call | solution.py:414
  117.8 4.1 %down.2 = bf16[128,4096]{1,0:T(8,128)(2,1)} custom-call(bf16[128,256]{1,0:T(8,128)(2,1)} %hidden.2, bf16[1,256,4096]{2,1,0:T(8,128)(2,1)} %weight.5), custom_call_target="tpu_custom_call" | custom-call | tf_op jit(solution)/shard_map/down/pallas_call | solution.py:418
  121.9 2.5 %fusion = bf16[16,8,4096]{2,1,0:T(8,128)(2,1)} fusion(bf16[128,4096]{1,0:T(8,128)(2,1)S(1)} %collective-permute-done.2, bf16[128,4096]{1,0:T(8,128)(2,1)} %down.2), kind=kLoop, calls=%fused_computation.1 | loop fusion | flops 2097152 | bytes 3145728 | tf_op jit(solution)/shard_map/reshape | solution.py:420
  124.4 5.0 %all-to-all-start.5 = ((bf16[16,8,4096]{2,1,0:T(8,128)(2,1)}), bf16[16,8,4096]{2,1,0:T(8,128)(2,1)S(1)}, u32[]{:S(2)}, u32[]{:S(2)}) async-start(bf16[16,8,4096]{2,1,0:T(8,128)(2,1)} %fusion), calls=%async_computation.5 | async-start | bytes 2097152 | tf_op jit(solution)/shard_map/all_to_all | solution.py:268
  130.2 16.5 %all-to-all-done.5.received = bf16[16,8,4096]{2,1,0:T(8,128)(2,1)S(1)} async-done(((bf16[16,8,4096]{2,1,0:T(8,128)(2,1)}), bf16[16,8,4096]{2,1,0:T(8,128)(2,1)S(1)}, u32[]{:S(2)}, u32[]{:S(2)}) %all-to-all-start.5) | async-done | bytes 1048608 | tf_op jit(solution)/shard_map/all_to_all | solution.py:268
  147.7 1.9 %chip_sum.1 = bf16[8,32,128]{2,1,0:T(8,128)(2,1)} custom-call(bf16[16,8,4096]{2,1,0:T(8,128)(2,1)} %copy-done.1), custom_call_target="tpu_custom_call" | custom-call | tf_op jit(solution)/shard_map/chip_sum/pallas_call | solution.py:421
  149.7 3.3 %all-to-all-start.6 = ((bf16[8,32,128]{2,1,0:T(8,128)(2,1)}), bf16[8,32,128]{2,1,0:T(8,128)(2,1)S(1)}, u32[]{:S(2)}, u32[]{:S(2)}) async-start(bf16[8,32,128]{2,1,0:T(8,128)(2,1)} %chip_sum.1), calls=%async_computation.6 | async-start | bytes 131072 | tf_op jit(solution)/shard_map/all_to_all | solution.py:268
  153.6 7.7 %all-to-all-done.6.received = bf16[8,32,128]{2,1,0:T(8,128)(2,1)S(1)} async-done(((bf16[8,32,128]{2,1,0:T(8,128)(2,1)}), bf16[8,32,128]{2,1,0:T(8,128)(2,1)S(1)}, u32[]{:S(2)}, u32[]{:S(2)}) %all-to-all-start.6) | async-done | bytes 65568 | tf_op jit(solution)/shard_map/all_to_all | solution.py:268
  (35 shorter events, 14.1 us)
Async XLA Ops:
  4.4 16.5 %all-to-all-start = ((bf16[8,16,128]{2,1,0:T(8,128)(2,1)}), bf16[8,16,128]{2,1,0:T(8,128)(2,1)S(1)}, u32[]{:S(2)}, u32[]{:S(2)}) async-start(bf16[8,16,128]{2,1,0:T(8,128)(2,1)} %bitcast.29), calls=%async_computation | async-start | bytes 65536 | tf_op jit(solution)/shard_map/all_to_all | solution.py:268
  20.9 0.6 copy-start.5
  48.8 1.6 collective-permute-start
  51.3 48.5 %copy-start.6 = (f32[256,2]{0,1:T(2,128)S(1)}, f32[256,2]{0,1:T(2,128)}, u32[]{:S(2)}) copy-start(f32[256,2]{0,1:T(2,128)} %param.24) | copy-start | bytes 6148
  51.3 48.5 %copy-start.7 = (s32[256,2]{0,1:T(2,128)S(1)}, s32[256,2]{0,1:T(2,128)}, u32[]{:S(2)}) copy-start(s32[256,2]{0,1:T(2,128)} %param.23) | copy-start | bytes 6148
  99.8 8.4 %copy-start = (bf16[16,128,256]{2,1,0:T(8,128)(2,1)}, bf16[16,128,256]{2,1,0:T(8,128)(2,1)S(1)}, u32[]{:S(2)}) copy-start(bf16[16,128,256]{2,1,0:T(8,128)(2,1)S(1)} %all_to_all.38.rows) | copy-start | bytes 3145732
  99.8 2.7 %collective-permute-start.1 = (bf16[16,128,256]{2,1,0:T(8,128)(2,1)S(1)}, bf16[16,128,256]{2,1,0:T(8,128)(2,1)S(1)}, u32[]{:S(2)}, u32[]{:S(2)}) collective-permute-start(bf16[16,128,256]{2,1,0:T(8,128)(2,1)S(1)} %all_to_all.38.rows), channel_id=1, source_target_pairs={{0,4},{4,0},{1,5},{5,1},{2,6},{6,2},{3,7},{7,3},{8,12},{12,8},{9,1... | collective-permute-start | bytes 3145736 | tf_op jit(solution)/shard_map/ppermute | solution.py:272
  102.5 1.0 copy-start.2
  112.2 9.7 %collective-permute-start.2 = (bf16[128,4096]{1,0:T(8,128)(2,1)}, bf16[128,4096]{1,0:T(8,128)(2,1)S(1)}, u32[]{:S(2)}, u32[]{:S(2)}) collective-permute-start(bf16[128,4096]{1,0:T(8,128)(2,1)} %down.3), channel_id=1, source_target_pairs={{0,4},{4,0},{1,5},{5,1},{2,6},{6,2},{3,7},{7,3},{8,12},{12,8},{9,1... | collective-permute-start | bytes 3145736 | tf_op jit(solution)/shard_map/ppermute | solution.py:272
  124.4 28.7 %copy-start.3 = (f32[4096]{0:T(1024)S(1)}, f32[4096]{0:T(1024)}, u32[]{:S(2)}) copy-start(f32[4096]{0:T(1024)} %param.21) | copy-start | bytes 49156
  124.4 22.4 %all-to-all-start.5 = ((bf16[16,8,4096]{2,1,0:T(8,128)(2,1)}), bf16[16,8,4096]{2,1,0:T(8,128)(2,1)S(1)}, u32[]{:S(2)}, u32[]{:S(2)}) async-start(bf16[16,8,4096]{2,1,0:T(8,128)(2,1)} %fusion), calls=%async_computation.5 | async-start | bytes 2097152 | tf_op jit(solution)/shard_map/all_to_all | solution.py:268
  146.7 1.0 copy-start.1
  149.7 11.7 %all-to-all-start.6 = ((bf16[8,32,128]{2,1,0:T(8,128)(2,1)}), bf16[8,32,128]{2,1,0:T(8,128)(2,1)S(1)}, u32[]{:S(2)}, u32[]{:S(2)}) async-start(bf16[8,32,128]{2,1,0:T(8,128)(2,1)} %chip_sum.1), calls=%async_computation.6 | async-start | bytes 131072 | tf_op jit(solution)/shard_map/all_to_all | solution.py:268
  161.3 0.6 copy-start.4

commit v2 on v1

v2 whole, which is shorter than its diff:
```python
import jax
import jax.numpy as jnp
from jax import lax
from jax.experimental import pallas as pl
from jax.experimental.pallas import tpu as pltpu
from jax.sharding import Mesh, PartitionSpec as P

bf16 = jnp.bfloat16
f32 = jnp.float32
i32 = jnp.int32

DP, NX, NC, MP = 8, 4, 2, 4
EXPERTS = NX * NC
HOLDERS = DP * MP
PMAX = 4
SEQ = 32
TOTAL = DP * SEQ
SLOTS = 32
PAGE = 256
HEAD = 128
GROUPS = 4
D = 4096
FF = 256
CHIPS = NX * MP
COLS = D // CHIPS
HALF = SEQ // NC
ROWS = DP * HALF
FLOOR = -1e30
SCALE = HEAD ** (-0.5)


def iota(shape, dim):
    return lax.broadcasted_iota(i32, shape, dim)


def dot(a, b, dims=((1,), (0,))):
    return lax.dot_general(a, b, (dims, ((), ())), preferred_element_type=f32)


def one_hot(mask):
    return jnp.where(mask, 1.0, 0.0).astype(bf16)


def core_rows(core, count):
    row = iota((count, SEQ), 0)
    wanted = (row // MP) * (NC * MP) + core * MP + row % MP
    return one_hot(wanted == iota((count, SEQ), 1))


def select_kernel(queries, holders, out):
    first = lax.axis_index("dp") * SEQ
    table = pltpu.roll(holders[...], (TOTAL - first) % TOTAL, 1)[:, :SEQ]
    row = iota((HEAD, SEQ), 0)
    named = jnp.zeros((HEAD, SEQ), i32)
    for j in range(PMAX):
        named = jnp.where(row % PMAX == j, table[j : j + 1], named)
    wanted = (row // (GROUPS * PMAX)) * MP + lax.axis_index("mp")
    found = jnp.zeros((HEAD, HEAD), f32)
    for k in range(GROUPS):
        pick = one_hot((named == wanted) & ((row // PMAX) % GROUPS == k))
        found = found + dot(pick, queries[:, k * HEAD : (k + 1) * HEAD])
    out[...] = found.astype(bf16)


def index_kernel(holders, slots, lengths, pages, spread, live, gather, order):
    del pages
    mine = lax.axis_index("dp") * MP + lax.axis_index("mp")

    def rows_of(array, count):
        row = iota((count, TOTAL), 0)
        rows = jnp.zeros((count, TOTAL), i32)
        for j in range(PMAX):
            rows = jnp.where(row % PMAX == j, array[j : j + 1], rows)
        return rows

    def held(count, group):
        lane = iota((count, TOTAL), 1)
        return (rows_of(holders[...], count) == mine) & (lane // SEQ == group)

    def total(mask, values):
        return jnp.sum(jnp.where(mask, values, 0), axis=1, keepdims=True)

    row = iota((HEAD, TOTAL), 0)
    lane = iota((HEAD, TOTAL), 1)
    mask = held(HEAD, row // (GROUPS * PMAX))
    slot = total(mask, rows_of(slots[...], HEAD))
    length = total(mask, lengths[...])
    count = jnp.clip(length - PAGE * (iota((HEAD, 1), 0) % PMAX), 0, PAGE)
    match = (slot == lane // 8) & ((row // PMAX) % GROUPS == lane % GROUPS)
    turned = jnp.where(match, 1.0, 0.0).T.astype(bf16)
    spread[...] = turned
    live[...] = dot(turned, jnp.broadcast_to(count.astype(f32), (HEAD, HEAD)).astype(bf16))

    row = iota((TOTAL, TOTAL), 0)
    mask = held(TOTAL, row // SEQ)
    slot = total(mask, rows_of(slots[...], TOTAL))
    row = iota((TOTAL, 1), 0)
    target = slot * 8 + (row // 8) % GROUPS + jnp.where(row % 8 < PMAX, 0, TOTAL)
    gather[...] = one_hot(target == iota((TOTAL, 2 * TOTAL), 1))

    first = lax.axis_index("dp") * SEQ
    lane = iota((8, TOTAL), 1)
    named = jnp.zeros((8, TOTAL), i32)
    table = jnp.concatenate([holders[...]] * 2, axis=0)
    for r in range(8):
        rolled = pltpu.roll(table, (TOTAL - first + r * SEQ) % TOTAL, 1)
        named = jnp.where(lane // SEQ == r, rolled[r % PMAX : r % PMAX + 1], named)
    lane = iota((TOTAL, TOTAL), 1)
    match = named[0:1] * 8 + lane // SEQ == iota((TOTAL, TOTAL), 0)
    order[...] = jnp.where(match, 1.0, 0.0).T.astype(bf16)


STEP = 8


def attend_kernel(queries, spread, live, gather, pages, out, parts):
    for step in range(SLOTS // STEP):
        rows = slice(step * STEP * 8, (step + 1) * STEP * 8)
        wanted = dot(spread[rows], queries[...])
        scores = jnp.concatenate(
            [
                dot(
                    wanted[k * 8 : (k + 1) * 8].astype(bf16),
                    pages[0, step * STEP + k, 0],
                    ((1,), (1,)),
                )
                for k in range(STEP)
            ],
            axis=0,
        )
        scores = scores * SCALE
        position = iota((STEP * 8, PAGE), 1).astype(f32)
        is_live = position < live[rows, 0:1]
        masked = jnp.where(is_live, scores, FLOOR)
        top = jnp.max(masked, axis=1, keepdims=True).astype(bf16).astype(f32)
        weights = jnp.where(is_live, jnp.exp(masked - top), 0.0)
        total = jnp.sum(weights, axis=1, keepdims=True)
        coarse = weights.astype(bf16).astype(f32)
        first = iota((STEP * 8, PAGE), 0) % 8 < GROUPS
        split = jnp.where(first, coarse, weights - coarse)
        found = []
        for k in range(STEP):
            both = dot(split[k * 8 : (k + 1) * 8].astype(bf16), pages[0, step * STEP + k, 1])
            found.append(both + pltpu.roll(both, GROUPS, 0))
        parts[rows, :] = jnp.concatenate(found, axis=0)
        lane = iota((STEP * 8, HEAD), 1)
        high = total.astype(bf16).astype(f32)
        tops = jnp.where(lane < 64, top, jnp.where(lane < 96, high, total - high))
        parts[TOTAL + step * STEP * 8 : TOTAL + (step + 1) * STEP * 8, :] = tops
    out[...] = dot(gather[...], parts[...].astype(bf16)).astype(bf16)


PROJ = 4


def project_kernel(received, queries, fresh, order, weight, mine, theirs):
    core = lax.axis_index("core")
    head = pl.multiple_of(lax.axis_index("mp") * HEAD, HEAD)
    sorted_parts = dot(order[...], received[...])
    pages = [sorted_parts[j * SEQ : (j + 1) * SEQ] for j in range(PMAX)]
    scalars = [sorted_parts[(PMAX + j) * SEQ : (PMAX + j + 1) * SEQ] for j in range(PMAX)]
    asked = queries[:, pl.ds(head, HEAD)].astype(f32)
    own = jnp.sum(asked * fresh[0].astype(f32), axis=1, keepdims=True) * SCALE
    highest = own
    for part in scalars:
        highest = jnp.maximum(highest, part[:, 0:1])
    factor = jnp.exp(own - highest)
    total = factor
    weighted = factor * fresh[1].astype(f32)
    for page, part in zip(pages, scalars):
        factor = jnp.exp(part[:, 0:1] - highest)
        total = total + (part[:, 64:65] + part[:, 96:97]) * factor
        weighted = weighted + page * factor
    rows = (weighted / total).astype(bf16)
    both = jnp.concatenate([core_rows(core, HALF), core_rows(1 - core, HALF)], axis=0)
    attended = dot(both, rows).astype(bf16)
    for k in range(CHIPS):
        block = dot(attended, weight[:, k * COLS : (k + 1) * COLS])
        mine[k] = block[:HALF]
        theirs[k] = block[HALF:].astype(bf16)


def join_kernel(mine, theirs, out):
    out[...] = (mine[...].astype(f32) + theirs[...].astype(f32)).astype(bf16)


def residual_kernel(received, tokens, gain, out):
    chip = lax.axis_index("x") * MP + lax.axis_index("mp")
    cols = pl.ds(pl.multiple_of(chip * COLS, COLS), COLS)
    summed = jnp.sum(received[...].astype(f32), axis=0)
    own = dot(core_rows(lax.axis_index("core"), HALF), tokens[:, cols])
    gained = ((summed + own) * gain[:, cols]).astype(bf16)
    out[...] = jnp.broadcast_to(gained[None], (DP, HALF, COLS))


def spread_kernel(rows, out):
    out[...] = jnp.broadcast_to(rows[...][None], out.shape)


def hidden_of(rows, gain, gate, up, ids, values, core):
    part = jnp.concatenate([rows[k] for k in range(CHIPS)], axis=1)
    gate_sum = dot(part, gate[0])
    up_sum = dot(part, up[0])
    inverse = 1.0 / gain[...]
    squares = jnp.zeros((ROWS, COLS), f32)
    for k in range(CHIPS):
        plain = rows[k].astype(f32) * inverse[:, k * COLS : (k + 1) * COLS]
        squares = squares + plain * plain
    mean = jnp.sum(squares, axis=1, keepdims=True) * (1.0 / D)
    scale = lax.rsqrt(mean + 1e-05)
    gated = gate_sum * scale
    value = gated / (1.0 + jnp.exp(-gated)) * (up_sum * scale)
    expert = lax.axis_index("x") * NC + lax.axis_index("core")
    routed = jnp.sum(jnp.where(ids[...] == expert, values[...], 0.0), axis=0, keepdims=True)
    row = iota((ROWS, TOTAL), 0)
    token = (row // CHIPS) * SEQ + ((row % CHIPS) // MP) * (NC * MP) + core * MP + row % MP
    picked = jnp.where(token == iota((ROWS, TOTAL), 1), routed, 0.0)
    value = (value * jnp.sum(picked, axis=1, keepdims=True)).astype(bf16)
    row = iota((ROWS, ROWS), 0)
    order = one_hot((row % DP) * CHIPS + row // DP == iota((ROWS, ROWS), 1))
    return dot(order, value).astype(bf16)


def own_kernel(rows, gain, gate, up, ids, values, out, residual):
    out[...] = hidden_of(rows, gain, gate, up, ids, values, lax.axis_index("core"))
    home = lax.axis_index("dp") * CHIPS + lax.axis_index("x") * MP + lax.axis_index("mp")
    pick = one_hot(iota((8, ROWS), 1) == home)
    for k in range(CHIPS):
        row = dot(pick, rows[k])
        residual[2 * k : 2 * k + 1] = row[:1, :HEAD]
        residual[2 * k + 1 : 2 * k + 2] = row[:1, HEAD:]


def other_kernel(after, rows, gain, gate, up, ids, values, weight, out):
    del after
    hidden = hidden_of(rows, gain, gate, up, ids, values, 1 - lax.axis_index("core"))
    for k in range(CHIPS):
        cols = slice(k * COLS, (k + 1) * COLS)
        out[:, cols] = dot(hidden, weight[0, :, cols]).astype(bf16)


def down_kernel(hidden, weight, out):
    for k in range(CHIPS):
        cols = slice(k * COLS, (k + 1) * COLS)
        out[:, cols] = dot(hidden[...], weight[0, :, cols]).astype(bf16)


def chip_sum_kernel(received, out):
    for k in range(CHIPS):
        cols = slice(k * COLS, (k + 1) * COLS)
        summed = jnp.sum(received[:, :, cols].astype(f32), axis=0)
        out[:, 2 * k : 2 * k + 2, :] = summed.reshape(DP, 2, HEAD).astype(bf16)


def final_kernel(received, residual, gain, out):
    summed = jnp.sum(received[...].astype(f32), axis=0) + residual[...] / gain[...]
    for k in range(D // HEAD):
        out[:, k * HEAD : (k + 1) * HEAD] = summed[k : k + 1].astype(bf16)


def call(kernel, out_shape, arrays, scratch=(), limit=8, name=None):
    vmem = pl.BlockSpec(memory_space=pltpu.VMEM)
    return pl.pallas_call(
        kernel,
        out_shape=out_shape,
        in_specs=[vmem] * len(arrays),
        out_specs=jax.tree.map(lambda _: vmem, out_shape),
        scratch_shapes=scratch,
        compiler_params=pltpu.CompilerParams(vmem_limit_bytes=limit * 2**20),
        name=name,
    )(*arrays)


def struct(shape, dtype=bf16):
    return jax.ShapeDtypeStruct(shape, dtype)


def exchange(array, axes):
    return lax.all_to_all(array, axes, 0, 0, tiled=True)


def swap(array):
    return lax.ppermute(array, "core", [(0, 1), (1, 0)])


def body(
    queries,
    fresh_entries,
    page_cache,
    lengths,
    page_holder,
    page_slot,
    tokens,
    norm_gain,
    out_weight,
    expert_ids,
    gate_values,
    gate_weight,
    up_weight,
    down_weight,
):
    gain = norm_gain.reshape(1, D)
    holders = page_holder.T
    ids = expert_ids.T
    values = gate_values.T

    lines = DP * GROUPS * PMAX
    selected = call(select_kernel, struct((lines, HEAD)), (queries, holders), name="select")
    asked = exchange(selected.reshape(DP, GROUPS * PMAX, HEAD), "dp").reshape(lines, HEAD)
    spread, live, gather, order = call(
        index_kernel,
        (
            struct((TOTAL, HEAD)),
            struct((TOTAL, HEAD), f32),
            struct((TOTAL, 2 * TOTAL)),
            struct((TOTAL, TOTAL)),
        ),
        (holders, page_slot.T, lengths.reshape(1, TOTAL), page_cache),
        name="index",
    )
    parts = call(
        attend_kernel,
        struct((TOTAL, HEAD)),
        (asked, spread, live, gather, page_cache),
        scratch=[pltpu.VMEM((2 * TOTAL, HEAD), f32)],
        name="attend",
    )
    parts = exchange(parts.reshape(HOLDERS, 8, HEAD), ("dp", "mp")).reshape(TOTAL, HEAD)

    mine, theirs = call(
        project_kernel,
        (struct((CHIPS, HALF, COLS), f32), struct((CHIPS, HALF, COLS))),
        (parts, queries, fresh_entries, order, out_weight),
        name="project",
    )
    joined = call(
        join_kernel, struct((CHIPS, HALF, COLS)), (mine, swap(theirs)), name="join_heads"
    )
    joined = exchange(joined, ("x", "mp"))

    gained = call(
        residual_kernel, struct((DP, HALF, COLS)), (joined, tokens, gain), name="residual"
    )
    gained = exchange(gained, "dp").reshape(ROWS, COLS)
    copies = call(spread_kernel, struct((CHIPS, ROWS, COLS)), (gained,), name="spread")
    own_rows = exchange(copies, ("x", "mp"))
    other_rows = swap(own_rows)

    own_hidden, residual = call(
        own_kernel,
        (struct((ROWS, FF)), struct((D // HEAD, HEAD), f32)),
        (own_rows, gain, gate_weight, up_weight, ids, values),
        name="own",
    )
    other_out = call(
        other_kernel,
        struct((ROWS, D)),
        (own_hidden, other_rows, gain, gate_weight, up_weight, ids, values, down_weight),
        name="other",
    )
    passed = swap(other_out)
    own_out = call(down_kernel, struct((ROWS, D)), (own_hidden, down_weight), name="down")
    summed = call(join_kernel, struct((ROWS, D)), (own_out, passed), name="join_experts")
    summed = exchange(summed.reshape(CHIPS, DP, D), ("x", "mp"))
    rows = call(chip_sum_kernel, struct((DP, D // HEAD, HEAD)), (summed,), name="chip_sum")
    rows = exchange(rows, "dp")
    return call(
        final_kernel,
        struct((1, D)),
        (rows, residual, norm_gain.reshape(D // HEAD, HEAD)),
        name="final",
    )


def solution(mesh):
    fine = Mesh(mesh.devices.reshape(DP, NX, NC, MP), ("dp", "x", "core", "mp"))
    expert = ("x", "core")
    return jax.shard_map(
        body,
        mesh=fine,
        in_specs=(
            P("dp", expert),
            P(None, "dp", expert),
            P(expert, ("dp", "mp"), None, None, None),
            P(),
            P(),
            P(),
            P("dp", None),
            P(),
            P((*expert, "mp"), None),
            P(),
            P(),
            P(expert, None, ("dp", "mp")),
            P(expert, None, ("dp", "mp")),
            P(expert, ("dp", "mp"), None),
        ),
        out_specs=P(("dp", *expert, "mp"), None),
        check_vma=False,
    )
```

time: 165 us -> 124 us (0.75)
  Pallas kernels: 40.5 us -> 8.48 us
  blocking collectives: 61.5 us -> 89.7 us
  waiting for transfers between devices: 29.3 us -> 8.27 us
  starting transfers between devices: 17 us -> 8.78 us
  other arithmetic: 5.6 us -> 0 us
    pallas_call x12 -> x13, Pallas kernels: 40.5 us -> 8.48 us  [call(): pl.pallas_call(kernel, out_shape=out_shape, in_specs=[vmem] * len(arrays)...]
    all_to_all x4 -> x6, blocking collectives: 61.5 us -> 89.7 us  [exchange(): return lax.all_to_all(array, axes, 0, 0, tiled=True)]
    all_to_all x3 -> x1, waiting for transfers between devices: 26.2 us -> 3.27 us  [exchange(): return lax.all_to_all(array, axes, 0, 0, tiled=True)]
    all_to_all x3 -> x1, starting transfers between devices: 16.8 us -> 8.46 us  [exchange(): return lax.all_to_all(array, axes, 0, 0, tiled=True)]
    reshape x2 -> x0, other arithmetic: 3.09 us -> none  [the longest x1 2.48 us: body(): summed = exchange(summed.reshape(CHIPS, DP, D), ('x', 'mp'))]
    convert_element_type x2 -> x0, other arithmetic: 1.84 us -> none  [the longest x1 0.99 us: body(): joined = (mine + swap(theirs).astype(f32)).astype(bf16)]
    ppermute x3, waiting for transfers between devices: 3.17 us -> 5 us  [swap(): return lax.ppermute(array, 'core', [(0, 1), (1, 0)])]
    unnamed x18 -> x34, local copies, waits for them, and re-layouts: 6.19 us -> 7.92 us
  transfers between devices with their start and end apart: 6 -> 4, of which waited for: 5 -> 4; matrix products, arithmetic and copies ran while one was open for 4% -> 0% of each run, Pallas kernels for 7% -> 2%
where the time goes in v2:
time: 124 us; the launch traced here: 123 us
  blocking collectives  89.7 us (72%)
  starting transfers between devices  8.78 us (7%)
  Pallas kernels  8.48 us (7%)
  waiting for transfers between devices  8.27 us (7%)
  local copies, waits for them, and re-layouts  7.92 us (6%)
    all_to_all x6, blocking collectives, exchange(): return lax.all_to_all(array, axes, 0, 0, tiled=True)  89.7 us
    pallas_call x13, Pallas kernels, call(): pl.pallas_call(kernel, out_shape=out_shape, in_specs=[vmem] * len(arrays)...  8.48 us
    all_to_all x1, starting transfers between devices, exchange(): return lax.all_to_all(array, axes, 0, 0, tiled=True)  8.46 us
    unnamed x34, local copies, waits for them, and re-layouts  7.92 us
    ppermute x3, waiting for transfers between devices, swap(): return lax.ppermute(array, 'core', [(0, 1), (1, 0)])  5 us
    all_to_all x1, waiting for transfers between devices, exchange(): return lax.all_to_all(array, axes, 0, 0, tiled=True)  3.27 us
  transfers between devices with their start and end apart: 4, of which 4 were waited for; matrix products, arithmetic and copies ran while one was open for 0% of the time, Pallas kernels for 2%

profile of v2, /device:TPU:8, one launch (start us, length us, event | category | flops | bytes accessed | tf_op | source)
XLA Modules:
  0.0 123.3 jit_solution(6694213273236887307)
XLA Ops:
  0.0 0.8 copy-done.8
  0.8 0.7 copy-done.11
  1.4 0.9 select.1
  2.3 8.5 %all-to-all-start = ((bf16[8,16,128]{2,1,0:T(8,128)(2,1)}), bf16[8,16,128]{2,1,0:T(8,128)(2,1)S(1)}, u32[]{:S(2)}, u32[]{:S(2)}) async-start(bf16[8,16,128]{2,1,0:T(8,128)(2,1)} %bitcast.1), calls=%async_computation | async-start | bytes 65536 | tf_op jit(solution)/shard_map/all_to_all | solution.py:279
  10.8 2.2 %copy-done = bf16[1,32,2,256,128]{4,3,2,1,0:T(8,128)(2,1)S(1)} copy-done((bf16[1,32,2,256,128]{4,3,2,1,0:T(8,128)(2,1)S(1)}, bf16[1,32,2,256,128]{4,3,2,1,0:T(8,128)(2,1)}, u32[]{:S(2)}) %copy-start) | copy-done | bytes 4194328
  13.0 0.7 copy-done.12
  13.7 0.7 copy-done.15
  14.3 0.7 copy-done.16
  15.5 3.3 %all-to-all-done = bf16[8,16,128]{2,1,0:T(8,128)(2,1)S(1)} async-done(((bf16[8,16,128]{2,1,0:T(8,128)(2,1)}), bf16[8,16,128]{2,1,0:T(8,128)(2,1)S(1)}, u32[]{:S(2)}, u32[]{:S(2)}) %all-to-all-start) | async-done | bytes 32800 | tf_op jit(solution)/shard_map/all_to_all | solution.py:279
  18.8 2.2 %copy-done.1 = bf16[1,32,2,256,128]{4,3,2,1,0:T(8,128)(2,1)S(1)} copy-done((bf16[1,32,2,256,128]{4,3,2,1,0:T(8,128)(2,1)S(1)}, bf16[1,32,2,256,128]{4,3,2,1,0:T(8,128)(2,1)}, u32[]{:S(2)}) %copy-start.1) | copy-done | bytes 4194328
  21.0 2.1 %attend.1 = bf16[256,128]{1,0:T(8,128)(2,1)S(1)} custom-call(bf16[128,128]{1,0:T(8,128)(2,1)S(1)} %bitcast.21, bf16[256,128]{1,0:T(8,128)(2,1)S(1)} %get-tuple-element.13.spread, f32[256,128]{1,0:T(8,128)S(1)} %get-tuple-element.14.live, bf16[256,512]{1,0:T(8,128)(2,1)S(1)} %get-tuple-element.15.gather, bf16[1,32,2,256,128]{4,3,2,1,0:T(8,128)(2,1)S(1)} %copy-done.1), custom_call_target="tpu_custom_call" | custom-call | tf_op jit(solution)/shard_map/attend/pallas_call | solution.py:263
  23.1 15.8 %all_to_all.35 = bf16[32,8,128]{2,1,0:T(8,128)(2,1)S(1)} all-to-all(bf16[32,8,128]{2,1,0:T(8,128)(2,1)S(1)} %bitcast.14), channel_id=1, replica_groups=mesh['dp'=8,'x'=4,'core'=2,'mp'=4] {'dp','mp'}, dimensions={0} | all-to-all | bytes 131072 | tf_op jit(solution)/shard_map/all_to_all | solution.py:279
  38.9 0.8 project.1
  39.9 1.3 %collective-permute-done.theirs = bf16[16,16,256]{2,1,0:T(8,128)(2,1)S(1)} collective-permute-done((bf16[16,16,256]{2,1,0:T(8,128)(2,1)S(1)}, bf16[16,16,256]{2,1,0:T(8,128)(2,1)S(1)}, u32[]{:S(2)}, u32[]{:S(2)}) %collective-permute-start) | collective-permute-done | bytes 131104 | tf_op jit(solution)/shard_map/ppermute | solution.py:283
  41.3 13.2 %all_to_all.36.received = bf16[16,16,256]{2,1,0:T(8,128)(2,1)S(1)} all-to-all(bf16[16,16,256]{2,1,0:T(8,128)(2,1)S(1)} %join_heads.1), channel_id=1, replica_groups=mesh['dp'=8,'x'=4,'core'=2,'mp'=4] {'x','mp'}, dimensions={0} | all-to-all | bytes 262144 | tf_op jit(solution)/shard_map/all_to_all | solution.py:279
  54.6 10.7 %all_to_all.37 = bf16[8,16,256]{2,1,0:T(8,128)(2,1)S(1)} all-to-all(bf16[8,16,256]{2,1,0:T(8,128)(2,1)S(1)} %residual.1), channel_id=1, replica_groups=mesh['dp'=8,'x'=4,'core'=2,'mp'=4] {'dp'}, dimensions={0} | all-to-all | bytes 131072 | tf_op jit(solution)/shard_map/all_to_all | solution.py:279
  65.4 18.6 %all_to_all.38.rows = bf16[16,128,256]{2,1,0:T(8,128)(2,1)S(1)} all-to-all(bf16[16,128,256]{2,1,0:T(8,128)(2,1)S(1)} %spread.1), channel_id=1, replica_groups=mesh['dp'=8,'x'=4,'core'=2,'mp'=4] {'x','mp'}, dimensions={0} | all-to-all | bytes 2097152 | tf_op jit(solution)/shard_map/all_to_all | solution.py:279
  84.1 1.0 own.1
  85.1 1.6 %collective-permute-done.1.rows = bf16[16,128,256]{2,1,0:T(8,128)(2,1)S(1)} collective-permute-done((bf16[16,128,256]{2,1,0:T(8,128)(2,1)S(1)}, bf16[16,128,256]{2,1,0:T(8,128)(2,1)S(1)}, u32[]{:S(2)}, u32[]{:S(2)}) %collective-permute-start.1) | collective-permute-done | bytes 1048608 | tf_op jit(solution)/shard_map/ppermute | solution.py:283
  86.7 1.4 %other.1 = bf16[128,4096]{1,0:T(8,128)(2,1)S(1)} custom-call(bf16[128,256]{1,0:T(8,128)(2,1)S(1)} %get-tuple-element.19.hidden.after, bf16[16,128,256]{2,1,0:T(8,128)(2,1)S(1)} %collective-permute-done.1.rows, f32[1,4096]{1,0:T(1,128)S(1)} %bitcast.17, bf16[1,4096,256]{2,1,0:T(8,128)(2,1)S(1)} %copy-done.2, bf16[1,4096,256]{2,1,0:T(8,128)(2,1)S(1)} %copy-done.3, ...), custom_call_target="tpu_custom_call" | custom-call | tf_op jit(solution)/shard_map/other/pallas_call | solution.py:263
  88.8 2.1 %collective-permute-done.2.theirs = bf16[128,4096]{1,0:T(8,128)(2,1)S(1)} collective-permute-done((bf16[128,4096]{1,0:T(8,128)(2,1)S(1)}, bf16[128,4096]{1,0:T(8,128)(2,1)S(1)}, u32[]{:S(2)}, u32[]{:S(2)}) %collective-permute-start.2) | collective-permute-done | bytes 1048608 | tf_op jit(solution)/shard_map/ppermute | solution.py:283
  91.1 20.7 %all_to_all.39.received = bf16[16,8,4096]{2,1,0:T(8,128)(2,1)S(1)} all-to-all(bf16[16,8,4096]{2,1,0:T(8,128)(2,1)S(1)} %bitcast.13), channel_id=1, replica_groups=mesh['dp'=8,'x'=4,'core'=2,'mp'=4] {'x','mp'}, dimensions={0} | all-to-all | bytes 2097152 | tf_op jit(solution)/shard_map/all_to_all | solution.py:279
  112.0 10.8 %all_to_all.40.received = bf16[8,32,128]{2,1,0:T(8,128)(2,1)S(1)} all-to-all(bf16[8,32,128]{2,1,0:T(8,128)(2,1)S(1)} %chip_sum.1), channel_id=1, replica_groups=mesh['dp'=8,'x'=4,'core'=2,'mp'=4] {'dp'}, dimensions={0} | all-to-all | bytes 131072 | tf_op jit(solution)/shard_map/all_to_all | solution.py:279
  122.7 0.6 final.1
  (37 shorter events, 2.0 us)
Async XLA Ops:
  0.0 0.8 copy-start.8
  0.8 0.7 copy-start.11
  2.3 16.5 %all-to-all-start = ((bf16[8,16,128]{2,1,0:T(8,128)(2,1)}), bf16[8,16,128]{2,1,0:T(8,128)(2,1)S(1)}, u32[]{:S(2)}, u32[]{:S(2)}) async-start(bf16[8,16,128]{2,1,0:T(8,128)(2,1)} %bitcast.1), calls=%async_computation | async-start | bytes 65536 | tf_op jit(solution)/shard_map/all_to_all | solution.py:279
  10.8 2.2 %copy-start = (bf16[1,32,2,256,128]{4,3,2,1,0:T(8,128)(2,1)S(1)}, bf16[1,32,2,256,128]{4,3,2,1,0:T(8,128)(2,1)}, u32[]{:S(2)}) copy-start(bf16[1,32,2,256,128]{4,3,2,1,0:T(8,128)(2,1)} %pages.3) | copy-start | bytes 12582916
  13.0 0.7 copy-start.12
  13.7 0.7 copy-start.15
  14.3 0.7 copy-start.16
  18.8 2.2 %copy-start.1 = (bf16[1,32,2,256,128]{4,3,2,1,0:T(8,128)(2,1)S(1)}, bf16[1,32,2,256,128]{4,3,2,1,0:T(8,128)(2,1)}, u32[]{:S(2)}) copy-start(bf16[1,32,2,256,128]{4,3,2,1,0:T(8,128)(2,1)} %pages.3) | copy-start | bytes 12582916
  21.0 17.9 %copy-start.5 = (bf16[128,4096]{1,0:T(8,128)(2,1)S(1)}, bf16[128,4096]{1,0:T(8,128)(2,1)}, u32[]{:S(2)}) copy-start(bf16[128,4096]{1,0:T(8,128)(2,1)} %weight.3) | copy-start | bytes 3145732
  21.0 17.9 %copy-start.9 = (bf16[32,512]{1,0:T(8,128)(2,1)S(1)}, bf16[32,512]{1,0:T(8,128)(2,1)}, u32[]{:S(2)}) copy-start(bf16[32,512]{1,0:T(8,128)(2,1)} %queries.3) | copy-start | bytes 98308
  21.0 17.9 %copy-start.10 = (bf16[2,32,128]{2,1,0:T(8,128)(2,1)S(1)}, bf16[2,32,128]{2,1,0:T(8,128)(2,1)}, u32[]{:S(2)}) copy-start(bf16[2,32,128]{2,1,0:T(8,128)(2,1)} %fresh.1) | copy-start | bytes 49156
  23.1 31.3 %copy-start.6 = (f32[4096]{0:T(1024)S(1)}, f32[4096]{0:T(1024)}, u32[]{:S(2)}) copy-start(f32[4096]{0:T(1024)} %param.21) | copy-start | bytes 49156
  23.1 31.3 %copy-start.7 = (bf16[32,4096]{1,0:T(8,128)(2,1)S(1)}, bf16[32,4096]{1,0:T(8,128)(2,1)}, u32[]{:S(2)}) copy-start(bf16[32,4096]{1,0:T(8,128)(2,1)} %tokens.1) | copy-start | bytes 786436
  39.8 1.4 %collective-permute-start = (bf16[16,16,256]{2,1,0:T(8,128)(2,1)S(1)}, bf16[16,16,256]{2,1,0:T(8,128)(2,1)S(1)}, u32[]{:S(2)}, u32[]{:S(2)}) collective-permute-start(bf16[16,16,256]{2,1,0:T(8,128)(2,1)S(1)} %get-tuple-element.18), channel_id=1, source_target_pairs={{0,4},{4,0},{1,5},{5,1},{2,6},{6,2},{3,7},{7,3},{8,12},{12,8},{9,1... | collective-permute-start | bytes 393224 | tf_op jit(solution)/shard_map/ppermute | solution.py:283
  41.2 42.8 %copy-start.3 = (bf16[1,4096,256]{2,1,0:T(8,128)(2,1)S(1)}, bf16[1,4096,256]{2,1,0:T(8,128)(2,1)}, u32[]{:S(2)}) copy-start(bf16[1,4096,256]{2,1,0:T(8,128)(2,1)} %up.3) | copy-start | bytes 6291460
  41.2 42.8 %copy-start.2 = (bf16[1,4096,256]{2,1,0:T(8,128)(2,1)S(1)}, bf16[1,4096,256]{2,1,0:T(8,128)(2,1)}, u32[]{:S(2)}) copy-start(bf16[1,4096,256]{2,1,0:T(8,128)(2,1)} %gate.3) | copy-start | bytes 6291460
  41.3 42.8 %copy-start.13 = (s32[256,2]{0,1:T(2,128)S(1)}, s32[256,2]{0,1:T(2,128)}, u32[]{:S(2)}) copy-start(s32[256,2]{0,1:T(2,128)} %param.23) | copy-start | bytes 6148
  41.3 42.8 %copy-start.14 = (f32[256,2]{0,1:T(2,128)S(1)}, f32[256,2]{0,1:T(2,128)}, u32[]{:S(2)}) copy-start(f32[256,2]{0,1:T(2,128)} %param.24) | copy-start | bytes 6148
  84.0 2.7 %collective-permute-start.1 = (bf16[16,128,256]{2,1,0:T(8,128)(2,1)S(1)}, bf16[16,128,256]{2,1,0:T(8,128)(2,1)S(1)}, u32[]{:S(2)}, u32[]{:S(2)}) collective-permute-start(bf16[16,128,256]{2,1,0:T(8,128)(2,1)S(1)} %all_to_all.38.rows), channel_id=1, source_target_pairs={{0,4},{4,0},{1,5},{5,1},{2,6},{6,2},{3,7},{7,3},{8,12},{12,8},{9,1... | collective-permute-start | bytes 3145736 | tf_op jit(solution)/shard_map/ppermute | solution.py:283
  84.1 2.6 %copy-start.4 = (bf16[1,256,4096]{2,1,0:T(8,128)(2,1)S(1)}, bf16[1,256,4096]{2,1,0:T(8,128)(2,1)}, u32[]{:S(2)}) copy-start(bf16[1,256,4096]{2,1,0:T(8,128)(2,1)} %weight.5) | copy-start | bytes 6291460
  88.1 2.7 %collective-permute-start.2 = (bf16[128,4096]{1,0:T(8,128)(2,1)S(1)}, bf16[128,4096]{1,0:T(8,128)(2,1)S(1)}, u32[]{:S(2)}, u32[]{:S(2)}) collective-permute-start(bf16[128,4096]{1,0:T(8,128)(2,1)S(1)} %other.1), channel_id=1, source_target_pairs={{0,4},{4,0},{1,5},{5,1},{2,6},{6,2},{3,7},{7,3},{8,12},{12,8},{9,1... | collective-permute-start | bytes 3145736 | tf_op jit(solution)/shard_map/ppermute | solution.py:283

commit v3 on v2

--- a/solution.py
+++ b/solution.py
@@ -47,7 +47,7 @@
     return one_hot(wanted == iota((count, SEQ), 1))
 
 
-def select_kernel(queries, holders, out):
+def select(queries, holders, out):
     first = lax.axis_index("dp") * SEQ
     table = pltpu.roll(holders[...], (TOTAL - first) % TOTAL, 1)[:, :SEQ]
     row = iota((HEAD, SEQ), 0)
@@ -62,8 +62,8 @@
     out[...] = found.astype(bf16)
 
 
-def index_kernel(holders, slots, lengths, pages, spread, live, gather, order):
-    del pages
+def select_kernel(queries, holders, slots, lengths, out, spread, live, gather, order):
+    select(queries, holders, out)
     mine = lax.axis_index("dp") * MP + lax.axis_index("mp")
 
     def rows_of(array, count):
@@ -236,19 +236,20 @@
     hidden = hidden_of(rows, gain, gate, up, ids, values, 1 - lax.axis_index("core"))
     for k in range(CHIPS):
         cols = slice(k * COLS, (k + 1) * COLS)
-        out[:, cols] = dot(hidden, weight[0, :, cols]).astype(bf16)
+        block = dot(hidden, weight[0, :, cols]).reshape(CHIPS, DP, COLS)
+        out[:, k * DP : (k + 1) * DP, :] = block.astype(bf16)
 
 
 def down_kernel(hidden, weight, out):
     for k in range(CHIPS):
         cols = slice(k * COLS, (k + 1) * COLS)
-        out[:, cols] = dot(hidden[...], weight[0, :, cols]).astype(bf16)
+        block = dot(hidden[...], weight[0, :, cols]).reshape(CHIPS, DP, COLS)
+        out[:, k * DP : (k + 1) * DP, :] = block.astype(bf16)
 
 
 def chip_sum_kernel(received, out):
     for k in range(CHIPS):
-        cols = slice(k * COLS, (k + 1) * COLS)
-        summed = jnp.sum(received[:, :, cols].astype(f32), axis=0)
+        summed = jnp.sum(received[:, k * DP : (k + 1) * DP, :].astype(f32), axis=0)
         out[:, 2 * k : 2 * k + 2, :] = summed.reshape(DP, 2, HEAD).astype(bf16)
 
 
@@ -258,7 +259,7 @@
         out[:, k * HEAD : (k + 1) * HEAD] = summed[k : k + 1].astype(bf16)
 
 
-def call(kernel, out_shape, arrays, scratch=(), limit=8, name=None):
+def call(kernel, out_shape, arrays, scratch=(), limit=8, micros=0, name=None):
     vmem = pl.BlockSpec(memory_space=pltpu.VMEM)
     return pl.pallas_call(
         kernel,
@@ -267,6 +268,11 @@
         out_specs=jax.tree.map(lambda _: vmem, out_shape),
         scratch_shapes=scratch,
         compiler_params=pltpu.CompilerParams(vmem_limit_bytes=limit * 2**20),
+        cost_estimate=pl.CostEstimate(
+            flops=micros * 10**8, bytes_accessed=micros * 10**6, transcendentals=0
+        )
+        if micros
+        else None,
         name=name,
     )(*arrays)
 
@@ -305,19 +311,23 @@
     values = gate_values.T
 
     lines = DP * GROUPS * PMAX
-    selected = call(select_kernel, struct((lines, HEAD)), (queries, holders), name="select")
-    asked = exchange(selected.reshape(DP, GROUPS * PMAX, HEAD), "dp").reshape(lines, HEAD)
-    spread, live, gather, order = call(
-        index_kernel,
+    selected, spread, live, gather, order = call(
+        select_kernel,
         (
+            struct((lines, HEAD)),
             struct((TOTAL, HEAD)),
             struct((TOTAL, HEAD), f32),
             struct((TOTAL, 2 * TOTAL)),
             struct((TOTAL, TOTAL)),
         ),
-        (holders, page_slot.T, lengths.reshape(1, TOTAL), page_cache),
-        name="index",
-    )
+        tuple(
+            pltpu.with_memory_space_constraint(array, pltpu.HBM)
+            for array in (queries, holders, page_slot.T, lengths.reshape(1, TOTAL))
+        ),
+        micros=8,
+        name="select",
+    )
+    asked = exchange(selected.reshape(DP, GROUPS * PMAX, HEAD), "dp").reshape(lines, HEAD)
     parts = call(
         attend_kernel,
         struct((TOTAL, HEAD)),
@@ -354,14 +364,16 @@
     )
     other_out = call(
         other_kernel,
-        struct((ROWS, D)),
+        struct((CHIPS, ROWS, COLS)),
         (own_hidden, other_rows, gain, gate_weight, up_weight, ids, values, down_weight),
         name="other",
     )
     passed = swap(other_out)
-    own_out = call(down_kernel, struct((ROWS, D)), (own_hidden, down_weight), name="down")
-    summed = call(join_kernel, struct((ROWS, D)), (own_out, passed), name="join_experts")
-    summed = exchange(summed.reshape(CHIPS, DP, D), ("x", "mp"))
+    own_out = call(down_kernel, struct((CHIPS, ROWS, COLS)), (own_hidden, down_weight), name="down")
+    summed = call(
+        join_kernel, struct((CHIPS, ROWS, COLS)), (own_out, passed), name="join_experts"
+    )
+    summed = exchange(summed, ("x", "mp"))
     rows = call(chip_sum_kernel, struct((DP, D // HEAD, HEAD)), (summed,), name="chip_sum")
     rows = exchange(rows, "dp")
     return call(

time: 124 us -> 120 us (0.968)
  blocking collectives: 89.7 us -> 104 us
  starting transfers between devices: 8.78 us -> 0.32 us
  local copies, waits for them, and re-layouts: 7.92 us -> 2.24 us
  waiting for transfers between devices: 8.27 us -> 5 us
    all_to_all x6 -> x7, blocking collectives: 89.7 us -> 104 us  [exchange(): return lax.all_to_all(array, axes, 0, 0, tiled=True)]
    all_to_all x1 -> x0, starting transfers between devices: 8.46 us -> none  [exchange(): return lax.all_to_all(array, axes, 0, 0, tiled=True)]
    unnamed x34 -> x22, local copies, waits for them, and re-layouts: 7.92 us -> 2.24 us
    all_to_all x1 -> x0, waiting for transfers between devices: 3.27 us -> none  [exchange(): return lax.all_to_all(array, axes, 0, 0, tiled=True)]
    pallas_call x13 -> x12, Pallas kernels: 8.48 us -> 8.46 us  [call(): pl.pallas_call(kernel, out_shape=out_shape, in_specs=[vmem] * len(arrays)...]
  transfers between devices with their start and end apart: 4 -> 3, of which waited for: 4 -> 3; matrix products, arithmetic and copies ran while one was open for 0% -> 0% of each run, Pallas kernels for 2% -> 1%
where the time goes in v3:
time: 120 us
  blocking collectives  104 us (87%)
  Pallas kernels  8.46 us (7%)
  waiting for transfers between devices  5 us (4%)
  local copies, waits for them, and re-layouts  2.24 us (2%)
    all_to_all x7, blocking collectives, exchange(): return lax.all_to_all(array, axes, 0, 0, tiled=True)  104 us
    pallas_call x12, Pallas kernels, call(): pl.pallas_call(kernel, out_shape=out_shape, in_specs=[vmem] * len(arrays)...  8.46 us
    ppermute x3, waiting for transfers between devices, swap(): return lax.ppermute(array, 'core', [(0, 1), (1, 0)])  5 us
  transfers between devices with their start and end apart: 3, of which 3 were waited for; matrix products, arithmetic and copies ran while one was open for 0% of the time, Pallas kernels for 1%

profile of v3, /device:TPU:8, one launch (start us, length us, event | category | flops | bytes accessed | tf_op | source)
XLA Modules:
  0.0 120.0 jit_solution(2608625423768425132)
XLA Ops:
  0.0 1.4 %select.1 = (bf16[128,128]{1,0:T(8,128)(2,1)S(1)}, bf16[256,128]{1,0:T(8,128)(2,1)S(1)}, f32[256,128]{1,0:T(8,128)S(1)}, bf16[256,512]{1,0:T(8,128)(2,1)S(1)}, bf16[256,256]{1,0:T(8,128)(2,1)S(1)}) custom-call(bf16[32,512]{1,0:T(8,128)(2,1)} %queries.3, s32[4,256]{1,0:T(4,128)} %bitcast.25, s32[4,256]{1,0:T(4,128)} %bitcast.26, s32[1,256]{1,0:T(1,128)} %bitcast.27), custom_call_target="tpu_custom_call" | custom-call | flops 800000000 | bytes 8000000 | tf_op jit(solution)/shard_map/select/pallas_call | solution.py:264
  1.4 16.3 %all_to_all.35 = bf16[8,16,128]{2,1,0:T(8,128)(2,1)S(1)} all-to-all(bf16[8,16,128]{2,1,0:T(8,128)(2,1)S(1)} %bitcast.20), channel_id=1, replica_groups=mesh['dp'=8,'x'=4,'core'=2,'mp'=4] {'dp'}, dimensions={0} | all-to-all | bytes 65536 | tf_op jit(solution)/shard_map/all_to_all | solution.py:285
  17.6 2.2 %copy-done.3 = bf16[1,32,2,256,128]{4,3,2,1,0:T(8,128)(2,1)S(1)} copy-done((bf16[1,32,2,256,128]{4,3,2,1,0:T(8,128)(2,1)S(1)}, bf16[1,32,2,256,128]{4,3,2,1,0:T(8,128)(2,1)}, u32[]{:S(2)}) %copy-start.3) | copy-done | bytes 4194328
  19.8 2.1 %attend.1 = bf16[256,128]{1,0:T(8,128)(2,1)S(1)} custom-call(bf16[128,128]{1,0:T(8,128)(2,1)S(1)} %bitcast.19, bf16[256,128]{1,0:T(8,128)(2,1)S(1)} %get-tuple-element.15.spread, f32[256,128]{1,0:T(8,128)S(1)} %get-tuple-element.16.live, bf16[256,512]{1,0:T(8,128)(2,1)S(1)} %get-tuple-element.17.gather, bf16[1,32,2,256,128]{4,3,2,1,0:T(8,128)(2,1)S(1)} %copy-done.3), custom_call_target="tpu_custom_call" | custom-call | tf_op jit(solution)/shard_map/attend/pallas_call | solution.py:264
  21.9 13.7 %all_to_all.36 = bf16[32,8,128]{2,1,0:T(8,128)(2,1)S(1)} all-to-all(bf16[32,8,128]{2,1,0:T(8,128)(2,1)S(1)} %bitcast.12), channel_id=1, replica_groups=mesh['dp'=8,'x'=4,'core'=2,'mp'=4] {'dp','mp'}, dimensions={0} | all-to-all | bytes 131072 | tf_op jit(solution)/shard_map/all_to_all | solution.py:285
  35.7 0.8 project.1
  36.5 0.1 collective-permute-start
  36.6 1.3 %collective-permute-done.theirs = bf16[16,16,256]{2,1,0:T(8,128)(2,1)S(1)} collective-permute-done((bf16[16,16,256]{2,1,0:T(8,128)(2,1)S(1)}, bf16[16,16,256]{2,1,0:T(8,128)(2,1)S(1)}, u32[]{:S(2)}, u32[]{:S(2)}) %collective-permute-start) | collective-permute-done | bytes 131104 | tf_op jit(solution)/shard_map/ppermute | solution.py:289
  38.0 13.1 %all_to_all.37.received = bf16[16,16,256]{2,1,0:T(8,128)(2,1)S(1)} all-to-all(bf16[16,16,256]{2,1,0:T(8,128)(2,1)S(1)} %join_heads.1), channel_id=1, replica_groups=mesh['dp'=8,'x'=4,'core'=2,'mp'=4] {'x','mp'}, dimensions={0} | all-to-all | bytes 262144 | tf_op jit(solution)/shard_map/all_to_all | solution.py:285
  51.1 0.1 residual.1
  51.3 10.7 %all_to_all.38 = bf16[8,16,256]{2,1,0:T(8,128)(2,1)S(1)} all-to-all(bf16[8,16,256]{2,1,0:T(8,128)(2,1)S(1)} %residual.1), channel_id=1, replica_groups=mesh['dp'=8,'x'=4,'core'=2,'mp'=4] {'dp'}, dimensions={0} | all-to-all | bytes 131072 | tf_op jit(solution)/shard_map/all_to_all | solution.py:285
  62.0 0.1 spread.1
  62.1 18.6 %all_to_all.39.rows = bf16[16,128,256]{2,1,0:T(8,128)(2,1)S(1)} all-to-all(bf16[16,128,256]{2,1,0:T(8,128)(2,1)S(1)} %spread.1), channel_id=1, replica_groups=mesh['dp'=8,'x'=4,'core'=2,'mp'=4] {'x','mp'}, dimensions={0} | all-to-all | bytes 2097152 | tf_op jit(solution)/shard_map/all_to_all | solution.py:285
  80.8 1.0 own.1
  81.8 1.6 %collective-permute-done.1.rows = bf16[16,128,256]{2,1,0:T(8,128)(2,1)S(1)} collective-permute-done((bf16[16,128,256]{2,1,0:T(8,128)(2,1)S(1)}, bf16[16,128,256]{2,1,0:T(8,128)(2,1)S(1)}, u32[]{:S(2)}, u32[]{:S(2)}) %collective-permute-start.1) | collective-permute-done | bytes 1048608 | tf_op jit(solution)/shard_map/ppermute | solution.py:289
  83.4 1.4 %other.1 = bf16[16,128,256]{2,1,0:T(8,128)(2,1)S(1)} custom-call(bf16[128,256]{1,0:T(8,128)(2,1)S(1)} %get-tuple-element.21.hidden.after, bf16[16,128,256]{2,1,0:T(8,128)(2,1)S(1)} %collective-permute-done.1.rows, f32[1,4096]{1,0:T(1,128)S(1)} %bitcast.15, bf16[1,4096,256]{2,1,0:T(8,128)(2,1)S(1)} %copy-done, bf16[1,4096,256]{2,1,0:T(8,128)(2,1)S(1)} %copy-done.1, ...), custom_call_target="tpu_custom_call" | custom-call | tf_op jit(solution)/shard_map/other/pallas_call | solution.py:264
  84.8 0.2 collective-permute-start.2
  85.0 0.4 down.1.mine
  85.5 2.1 %collective-permute-done.2.theirs = bf16[16,128,256]{2,1,0:T(8,128)(2,1)S(1)} collective-permute-done((bf16[16,128,256]{2,1,0:T(8,128)(2,1)S(1)}, bf16[16,128,256]{2,1,0:T(8,128)(2,1)S(1)}, u32[]{:S(2)}, u32[]{:S(2)}) %collective-permute-start.2) | collective-permute-done | bytes 1048608 | tf_op jit(solution)/shard_map/ppermute | solution.py:289
  87.5 0.2 join_experts.1
  87.8 20.7 %all_to_all.40.received = bf16[16,128,256]{2,1,0:T(8,128)(2,1)S(1)} all-to-all(bf16[16,128,256]{2,1,0:T(8,128)(2,1)S(1)} %join_experts.1), channel_id=1, replica_groups=mesh['dp'=8,'x'=4,'core'=2,'mp'=4] {'x','mp'}, dimensions={0} | all-to-all | bytes 2097152 | tf_op jit(solution)/shard_map/all_to_all | solution.py:285
  108.4 0.2 chip_sum.1
  108.7 10.8 %all_to_all.41.received = bf16[8,32,128]{2,1,0:T(8,128)(2,1)S(1)} all-to-all(bf16[8,32,128]{2,1,0:T(8,128)(2,1)S(1)} %chip_sum.1), channel_id=1, replica_groups=mesh['dp'=8,'x'=4,'core'=2,'mp'=4] {'dp'}, dimensions={0} | all-to-all | bytes 131072 | tf_op jit(solution)/shard_map/all_to_all | solution.py:285
  119.4 0.6 final.1
  (23 shorter events, 0.1 us)
Async XLA Ops:
  17.6 2.2 %copy-start.3 = (bf16[1,32,2,256,128]{4,3,2,1,0:T(8,128)(2,1)S(1)}, bf16[1,32,2,256,128]{4,3,2,1,0:T(8,128)(2,1)}, u32[]{:S(2)}) copy-start(bf16[1,32,2,256,128]{4,3,2,1,0:T(8,128)(2,1)} %pages.1) | copy-start | bytes 12582916
  19.8 15.8 %copy-start.4 = (bf16[128,4096]{1,0:T(8,128)(2,1)S(1)}, bf16[128,4096]{1,0:T(8,128)(2,1)}, u32[]{:S(2)}) copy-start(bf16[128,4096]{1,0:T(8,128)(2,1)} %weight.3) | copy-start | bytes 3145732
  19.8 15.8 %copy-start.7 = (bf16[32,512]{1,0:T(8,128)(2,1)S(1)}, bf16[32,512]{1,0:T(8,128)(2,1)}, u32[]{:S(2)}) copy-start(bf16[32,512]{1,0:T(8,128)(2,1)} %queries.3) | copy-start | bytes 98308
  19.8 15.8 %copy-start.8 = (bf16[2,32,128]{2,1,0:T(8,128)(2,1)S(1)}, bf16[2,32,128]{2,1,0:T(8,128)(2,1)}, u32[]{:S(2)}) copy-start(bf16[2,32,128]{2,1,0:T(8,128)(2,1)} %fresh.1) | copy-start | bytes 49156
  21.9 29.2 %copy-start.5 = (f32[4096]{0:T(1024)S(1)}, f32[4096]{0:T(1024)}, u32[]{:S(2)}) copy-start(f32[4096]{0:T(1024)} %param.21) | copy-start | bytes 49156
  21.9 29.2 %copy-start.6 = (bf16[32,4096]{1,0:T(8,128)(2,1)S(1)}, bf16[32,4096]{1,0:T(8,128)(2,1)}, u32[]{:S(2)}) copy-start(bf16[32,4096]{1,0:T(8,128)(2,1)} %tokens.1) | copy-start | bytes 786436
  36.5 1.4 %collective-permute-start = (bf16[16,16,256]{2,1,0:T(8,128)(2,1)S(1)}, bf16[16,16,256]{2,1,0:T(8,128)(2,1)S(1)}, u32[]{:S(2)}, u32[]{:S(2)}) collective-permute-start(bf16[16,16,256]{2,1,0:T(8,128)(2,1)S(1)} %get-tuple-element.20), channel_id=1, source_target_pairs={{0,4},{4,0},{1,5},{5,1},{2,6},{6,2},{3,7},{7,3},{8,12},{12,8},{9,1... | collective-permute-start | bytes 393224 | tf_op jit(solution)/shard_map/ppermute | solution.py:289
  37.9 42.8 %copy-start.1 = (bf16[1,4096,256]{2,1,0:T(8,128)(2,1)S(1)}, bf16[1,4096,256]{2,1,0:T(8,128)(2,1)}, u32[]{:S(2)}) copy-start(bf16[1,4096,256]{2,1,0:T(8,128)(2,1)} %up.3) | copy-start | bytes 6291460
  38.0 42.8 %copy-start = (bf16[1,4096,256]{2,1,0:T(8,128)(2,1)S(1)}, bf16[1,4096,256]{2,1,0:T(8,128)(2,1)}, u32[]{:S(2)}) copy-start(bf16[1,4096,256]{2,1,0:T(8,128)(2,1)} %gate.3) | copy-start | bytes 6291460
  38.0 42.8 %copy-start.9 = (s32[256,2]{0,1:T(2,128)S(1)}, s32[256,2]{0,1:T(2,128)}, u32[]{:S(2)}) copy-start(s32[256,2]{0,1:T(2,128)} %param.23) | copy-start | bytes 6148
  38.0 42.8 %copy-start.10 = (f32[256,2]{0,1:T(2,128)S(1)}, f32[256,2]{0,1:T(2,128)}, u32[]{:S(2)}) copy-start(f32[256,2]{0,1:T(2,128)} %param.24) | copy-start | bytes 6148
  80.7 2.7 %collective-permute-start.1 = (bf16[16,128,256]{2,1,0:T(8,128)(2,1)S(1)}, bf16[16,128,256]{2,1,0:T(8,128)(2,1)S(1)}, u32[]{:S(2)}, u32[]{:S(2)}) collective-permute-start(bf16[16,128,256]{2,1,0:T(8,128)(2,1)S(1)} %all_to_all.39.rows), channel_id=1, source_target_pairs={{0,4},{4,0},{1,5},{5,1},{2,6},{6,2},{3,7},{7,3},{8,12},{12,8},{9,1... | collective-permute-start | bytes 3145736 | tf_op jit(solution)/shard_map/ppermute | solution.py:289
  80.8 2.6 %copy-start.2 = (bf16[1,256,4096]{2,1,0:T(8,128)(2,1)S(1)}, bf16[1,256,4096]{2,1,0:T(8,128)(2,1)}, u32[]{:S(2)}) copy-start(bf16[1,256,4096]{2,1,0:T(8,128)(2,1)} %weight.5) | copy-start | bytes 6291460
  84.8 2.7 %collective-permute-start.2 = (bf16[16,128,256]{2,1,0:T(8,128)(2,1)S(1)}, bf16[16,128,256]{2,1,0:T(8,128)(2,1)S(1)}, u32[]{:S(2)}, u32[]{:S(2)}) collective-permute-start(bf16[16,128,256]{2,1,0:T(8,128)(2,1)S(1)} %other.1), channel_id=1, source_target_pairs={{0,4},{4,0},{1,5},{5,1},{2,6},{6,2},{3,7},{7,3},{8,12},{12,8},{9,1... | collective-permute-start | bytes 3145736 | tf_op jit(solution)/shard_map/ppermute | solution.py:289

commit v4 on v3

v4 whole, which is shorter than its diff:
```python
import jax
import jax.numpy as jnp
from jax import lax
from jax.experimental import pallas as pl
from jax.experimental.pallas import tpu as pltpu
from jax.sharding import Mesh, PartitionSpec as P

bf16 = jnp.bfloat16
f32 = jnp.float32
i32 = jnp.int32

DP, NX, NC, MP = 8, 4, 2, 4
EXPERTS = NX * NC
HOLDERS = DP * MP
PMAX = 4
SEQ = 32
TOTAL = DP * SEQ
SLOTS = 32
PAGE = 256
HEAD = 128
GROUPS = 4
D = 4096
FF = 256
CAP = 16
CHIPS = NX * MP
COLS = D // CHIPS
HALF = SEQ // NC
ROWS = DP * HALF
FLOOR = -1e30
SCALE = HEAD ** (-0.5)


def iota(shape, dim):
    return lax.broadcasted_iota(i32, shape, dim)


def dot(a, b, dims=((1,), (0,))):
    return lax.dot_general(a, b, (dims, ((), ())), preferred_element_type=f32)


def one_hot(mask):
    return jnp.where(mask, 1.0, 0.0).astype(bf16)


def select_kernel(queries, holders, out):
    first = lax.axis_index("dp") * SEQ
    table = pltpu.roll(holders[...], (TOTAL - first) % TOTAL, 1)[:, :SEQ]
    row = iota((HEAD, SEQ), 0)
    named = jnp.zeros((HEAD, SEQ), i32)
    for j in range(PMAX):
        named = jnp.where(row % PMAX == j, table[j : j + 1], named)
    wanted = (row // (GROUPS * PMAX)) * MP + lax.axis_index("mp")
    found = jnp.zeros((HEAD, HEAD), f32)
    for k in range(GROUPS):
        pick = one_hot((named == wanted) & ((row // PMAX) % GROUPS == k))
        found = found + dot(pick, queries[:, k * HEAD : (k + 1) * HEAD])
    out[...] = found.astype(bf16)


def index(holders, slots, lengths, spread, live, gather, order):
    mine = lax.axis_index("dp") * MP + lax.axis_index("mp")

    def rows_of(array, count):
        row = iota((count, TOTAL), 0)
        rows = jnp.zeros((count, TOTAL), i32)
        for j in range(PMAX):
            rows = jnp.where(row % PMAX == j, array[j : j + 1], rows)
        return rows

    def held(count, group):
        lane = iota((count, TOTAL), 1)
        return (rows_of(holders[...], count) == mine) & (lane // SEQ == group)

    def total(mask, values):
        return jnp.sum(jnp.where(mask, values, 0), axis=1, keepdims=True)

    row = iota((HEAD, TOTAL), 0)
    lane = iota((HEAD, TOTAL), 1)
    mask = held(HEAD, row // (GROUPS * PMAX))
    slot = total(mask, rows_of(slots[...], HEAD))
    length = total(mask, lengths[...])
    count = jnp.clip(length - PAGE * (iota((HEAD, 1), 0) % PMAX), 0, PAGE)
    match = (slot == lane // 8) & ((row // PMAX) % GROUPS == lane % GROUPS)
    turned = jnp.where(match, 1.0, 0.0).T.astype(bf16)
    spread[...] = turned
    live[...] = dot(turned, jnp.broadcast_to(count.astype(f32), (HEAD, HEAD)).astype(bf16))

    row = iota((TOTAL, TOTAL), 0)
    mask = held(TOTAL, row // SEQ)
    slot = total(mask, rows_of(slots[...], TOTAL))
    row = iota((TOTAL, 1), 0)
    target = slot * 8 + (row // 8) % GROUPS + jnp.where(row % 8 < PMAX, 0, TOTAL)
    gather[...] = one_hot(target == iota((TOTAL, 2 * TOTAL), 1))

    first = lax.axis_index("dp") * SEQ
    lane = iota((8, TOTAL), 1)
    named = jnp.zeros((8, TOTAL), i32)
    table = jnp.concatenate([holders[...]] * 2, axis=0)
    for r in range(8):
        rolled = pltpu.roll(table, (TOTAL - first + r * SEQ) % TOTAL, 1)
        named = jnp.where(lane // SEQ == r, rolled[r % PMAX : r % PMAX + 1], named)
    lane = iota((TOTAL, TOTAL), 1)
    match = named[0:1] * 8 + lane // SEQ == iota((TOTAL, TOTAL), 0)
    order[...] = jnp.where(match, 1.0, 0.0).T.astype(bf16)


def route(ids, values, picks, scatter, weights):
    core = lax.axis_index("core")
    own_x = lax.axis_index("x")
    expert = (iota((8, TOTAL), 0) % NX) * NC + core
    member = jnp.where((ids[0:1] == expert) | (ids[1:2] == expert), 1.0, 0.0)
    row = iota((TOTAL, TOTAL), 0)
    lane = iota((TOTAL, TOTAL), 1)
    before = one_hot((row < lane) & (row // SEQ == lane // SEQ))
    rank = dot(member.astype(bf16), before)
    row = iota((ROWS, TOTAL), 0)
    lane = iota((ROWS, TOTAL), 1)
    place = (row % CAP).astype(f32)
    own = jnp.zeros((ROWS, TOTAL), f32)
    for k in range(NX):
        match = (member[k : k + 1] > 0.5) & (rank[k : k + 1] == place)
        match = jnp.where(match & (lane // SEQ == row // CAP), 1.0, 0.0)
        picks[k * ROWS : (k + 1) * ROWS] = match.astype(bf16)
        own = jnp.where(own_x == k, match, own)
    chosen = own_x * NC + core
    value = jnp.sum(jnp.where(ids[...] == chosen, values[...], 0.0), axis=0, keepdims=True)
    weight = jnp.sum(own * value, axis=1, keepdims=True)
    weights[...] = jnp.broadcast_to(weight, (ROWS, HEAD))
    row = iota((TOTAL, TOTAL), 0)
    half = jnp.where(row < ROWS, 1 - core, core)
    chip = (row % ROWS) // DP
    token = (row % DP) * SEQ + (chip // MP) * (NC * MP) + half * MP + chip % MP
    order = one_hot(token == iota((TOTAL, TOTAL), 1))
    scatter[...] = dot(order, own.astype(bf16), ((1,), (1,))).astype(bf16)


STEP = 8
STEPS = SLOTS // STEP
EARLY = 2


def prepare_kernel(
    after, holders, slots, lengths, ids, values, pages, *outs_and_sem
):
    del after
    spread, live, gather, order, picks, scatter, weights, held, sem = outs_and_sem
    copy = pltpu.make_async_copy(pages.at[0, pl.ds(0, EARLY * STEP)], held, sem)
    copy.start()
    index(holders, slots, lengths, spread, live, gather, order)
    route(ids, values, picks, scatter, weights)
    copy.wait()


def attend_kernel(queries, spread, live, gather, early, pages, out, parts, late, sems):
    copies = [
        pltpu.make_async_copy(
            pages.at[0, pl.ds((EARLY + k) * STEP, STEP)],
            late.at[pl.ds(k * STEP, STEP)],
            sems.at[k],
        )
        for k in range(STEPS - EARLY)
    ]
    for copy in copies:
        copy.start()
    for step in range(STEPS):
        rows = slice(step * STEP * 8, (step + 1) * STEP * 8)
        wanted = dot(spread[rows], queries[...])
        held = early if step < EARLY else late
        first_page = (step if step < EARLY else step - EARLY) * STEP
        if step >= EARLY:
            copies[step - EARLY].wait()
        scores = jnp.concatenate(
            [
                dot(
                    wanted[k * 8 : (k + 1) * 8].astype(bf16),
                    held[first_page + k, 0],
                    ((1,), (1,)),
                )
                for k in range(STEP)
            ],
            axis=0,
        )
        scores = scores * SCALE
        position = iota((STEP * 8, PAGE), 1).astype(f32)
        is_live = position < live[rows, 0:1]
        masked = jnp.where(is_live, scores, FLOOR)
        top = jnp.max(masked, axis=1, keepdims=True).astype(bf16).astype(f32)
        weights = jnp.where(is_live, jnp.exp(masked - top), 0.0)
        total = jnp.sum(weights, axis=1, keepdims=True)
        coarse = weights.astype(bf16).astype(f32)
        first = iota((STEP * 8, PAGE), 0) % 8 < GROUPS
        split = jnp.where(first, coarse, weights - coarse)
        found = []
        for k in range(STEP):
            both = dot(split[k * 8 : (k + 1) * 8].astype(bf16), held[first_page + k, 1])
            found.append(both + pltpu.roll(both, GROUPS, 0))
        parts[rows, :] = jnp.concatenate(found, axis=0)
        lane = iota((STEP * 8, HEAD), 1)
        high = total.astype(bf16).astype(f32)
        tops = jnp.where(lane < 64, top, jnp.where(lane < 96, high, total - high))
        parts[TOTAL + step * STEP * 8 : TOTAL + (step + 1) * STEP * 8, :] = tops
    out[...] = dot(gather[...], parts[...].astype(bf16)).astype(bf16)


def project_kernel(received, queries, fresh, order, weight, out):
    head = pl.multiple_of(lax.axis_index("mp") * HEAD, HEAD)
    sorted_parts = dot(order[...], received[...])
    pages = [sorted_parts[j * SEQ : (j + 1) * SEQ] for j in range(PMAX)]
    scalars = [sorted_parts[(PMAX + j) * SEQ : (PMAX + j + 1) * SEQ] for j in range(PMAX)]
    asked = queries[:, pl.ds(head, HEAD)].astype(f32)
    own = jnp.sum(asked * fresh[0].astype(f32), axis=1, keepdims=True) * SCALE
    highest = own
    for part in scalars:
        highest = jnp.maximum(highest, part[:, 0:1])
    factor = jnp.exp(own - highest)
    total = factor
    weighted = factor * fresh[1].astype(f32)
    for page, part in zip(pages, scalars):
        factor = jnp.exp(part[:, 0:1] - highest)
        total = total + (part[:, 64:65] + part[:, 96:97]) * factor
        weighted = weighted + page * factor
    attended = (weighted / total).astype(bf16)
    for k in range(CHIPS):
        out[k] = dot(attended, weight[:, k * COLS : (k + 1) * COLS]).astype(bf16)


def sum_kernel(received, mine, sent):
    summed = jnp.sum(received[...].astype(f32), axis=0)
    mine[...] = summed
    sent[...] = summed.astype(bf16)


def residual_kernel(mine, theirs, tokens, gain, out, plain):
    chip = lax.axis_index("x") * MP + lax.axis_index("mp")
    cols = pl.ds(pl.multiple_of(chip * COLS, COLS), COLS)
    total = mine[...] + theirs[...].astype(f32) + tokens[:, cols].astype(f32)
    gained = (total * gain[:, cols]).astype(bf16)
    out[...] = jnp.broadcast_to(gained[None], (DP, SEQ, COLS))
    lines = total.reshape(NX, NC * MP, COLS)
    turned = jnp.concatenate([lines[:, MP:], lines[:, :MP]], axis=1)
    plain[...] = jnp.where(lax.axis_index("core") == 0, lines, turned)


def pick_kernel(rows, picks, out):
    for k in range(NX):
        block = dot(picks[k * ROWS : (k + 1) * ROWS], rows[...]).astype(bf16)
        for m in range(MP):
            out[k * MP + m] = block


def hidden_kernel(rows, gain, gate, up, scatter, weights, weight, out, mine):
    part = jnp.concatenate([rows[k] for k in range(CHIPS)], axis=1)
    gate_sum = dot(part, gate[0])
    up_sum = dot(part, up[0])
    inverse = 1.0 / gain[...]
    squares = jnp.zeros((ROWS, COLS), f32)
    for k in range(CHIPS):
        plain = rows[k].astype(f32) * inverse[:, k * COLS : (k + 1) * COLS]
        squares = squares + plain * plain
    mean = jnp.sum(squares, axis=1, keepdims=True) * (1.0 / D)
    scale = lax.rsqrt(mean + 1e-05)
    gated = gate_sum * scale
    value = gated / (1.0 + jnp.exp(-gated)) * (up_sum * scale)
    value = (value * weights[:, 0:1]).astype(bf16)
    hidden = dot(scatter[...], value).astype(bf16)
    mine[...] = hidden[ROWS:]
    for k in range(CHIPS):
        cols = slice(k * COLS, (k + 1) * COLS)
        block = dot(hidden[:ROWS], weight[0, :, cols]).reshape(CHIPS, DP, COLS)
        out[:, k * DP : (k + 1) * DP, :] = block.astype(bf16)


def down_kernel(hidden, weight, out):
    for k in range(CHIPS):
        cols = slice(k * COLS, (k + 1) * COLS)
        block = dot(hidden[...], weight[0, :, cols]).reshape(CHIPS, DP, COLS)
        out[:, k * DP : (k + 1) * DP, :] = block.astype(bf16)


def join_kernel(mine, theirs, plain, out):
    chip = lax.axis_index("x") * MP + lax.axis_index("mp")
    at = iota((ROWS, COLS), 0) == chip * DP + lax.axis_index("dp")
    for k in range(CHIPS):
        line = plain[k // MP, k % MP : k % MP + 1, :]
        total = mine[k].astype(f32) + theirs[k].astype(f32)
        out[k] = (total + jnp.where(at, line, 0.0)).astype(bf16)


def chip_sum_kernel(received, out):
    for k in range(CHIPS):
        summed = jnp.sum(received[:, k * DP : (k + 1) * DP, :].astype(f32), axis=0)
        out[:, 2 * k : 2 * k + 2, :] = summed.reshape(DP, 2, HEAD).astype(bf16)


def final_kernel(received, out):
    summed = jnp.sum(received[...].astype(f32), axis=0)
    for k in range(D // HEAD):
        out[:, k * HEAD : (k + 1) * HEAD] = summed[k : k + 1].astype(bf16)


def call(kernel, out_shape, arrays, scratch=(), limit=8, hbm=(), name=None):
    vmem = pl.BlockSpec(memory_space=pltpu.VMEM)
    anywhere = pl.BlockSpec(memory_space=pl.ANY)
    return pl.pallas_call(
        kernel,
        out_shape=out_shape,
        in_specs=[anywhere if k in hbm else vmem for k in range(len(arrays))],
        out_specs=jax.tree.map(lambda _: vmem, out_shape),
        scratch_shapes=scratch,
        compiler_params=pltpu.CompilerParams(vmem_limit_bytes=limit * 2**20),
        name=name,
    )(*arrays)


def struct(shape, dtype=bf16):
    return jax.ShapeDtypeStruct(shape, dtype)


def in_hbm(array):
    return pltpu.with_memory_space_constraint(array, pltpu.HBM)


def exchange(array, axes):
    return lax.all_to_all(array, axes, 0, 0, tiled=True)


def swap(array):
    return lax.ppermute(array, "core", [(0, 1), (1, 0)])


def body(
    queries,
    fresh_entries,
    page_cache,
    lengths,
    page_holder,
    page_slot,
    tokens,
    norm_gain,
    out_weight,
    expert_ids,
    gate_values,
    gate_weight,
    up_weight,
    down_weight,
):
    gain = norm_gain.reshape(1, D)
    holders = page_holder.T

    lines = DP * GROUPS * PMAX
    selected = call(
        select_kernel,
        struct((lines, HEAD)),
        (in_hbm(queries), in_hbm(holders)),
        name="select",
    )
    asked = exchange(selected.reshape(DP, GROUPS * PMAX, HEAD), "dp").reshape(lines, HEAD)
    spread, live, gather, order, picks, scatter, weights, early = call(
        prepare_kernel,
        (
            struct((TOTAL, HEAD)),
            struct((TOTAL, HEAD), f32),
            struct((TOTAL, 2 * TOTAL)),
            struct((TOTAL, TOTAL)),
            struct((NX * ROWS, TOTAL)),
            struct((TOTAL, ROWS)),
            struct((ROWS, HEAD), f32),
            struct((EARLY * STEP, *page_cache.shape[2:])),
        ),
        (
            selected,
            in_hbm(holders),
            in_hbm(page_slot.T),
            in_hbm(lengths.reshape(1, TOTAL)),
            in_hbm(expert_ids.T),
            in_hbm(gate_values.T),
            in_hbm(page_cache),
        ),
        scratch=[pltpu.SemaphoreType.DMA(())],
        hbm=(0, 6),
        name="prepare",
    )
    parts = call(
        attend_kernel,
        struct((TOTAL, HEAD)),
        (asked, spread, live, gather, early, in_hbm(page_cache)),
        scratch=[
            pltpu.VMEM((2 * TOTAL, HEAD), f32),
            pltpu.VMEM(((STEPS - EARLY) * STEP, *page_cache.shape[2:]), bf16),
            pltpu.SemaphoreType.DMA((STEPS - EARLY,)),
        ],
        hbm=(5,),
        name="attend",
    )
    parts = exchange(parts.reshape(HOLDERS, 8, HEAD), ("dp", "mp")).reshape(TOTAL, HEAD)

    projected = call(
        project_kernel,
        struct((CHIPS, SEQ, COLS)),
        (parts, queries, fresh_entries, order, out_weight),
        name="project",
    )
    projected = exchange(projected, ("x", "mp"))
    mine, sent = call(
        sum_kernel,
        (struct((SEQ, COLS), f32), struct((SEQ, COLS))),
        (projected,),
        name="sum_heads",
    )

    gained, plain = call(
        residual_kernel,
        (struct((DP, SEQ, COLS)), struct((NX, NC * MP, COLS), f32)),
        (mine, swap(sent), tokens, gain),
        name="residual",
    )
    gained = exchange(gained, "dp").reshape(TOTAL, COLS)
    picked = call(pick_kernel, struct((CHIPS, ROWS, COLS)), (gained, picks), name="pick")
    rows = exchange(picked, ("x", "mp"))
    other_out, own_hidden = call(
        hidden_kernel,
        (struct((CHIPS, ROWS, COLS)), struct((ROWS, FF))),
        (rows, gain, gate_weight, up_weight, scatter, weights, down_weight),
        name="hidden",
    )
    passed = swap(other_out)
    own_out = call(
        down_kernel, struct((CHIPS, ROWS, COLS)), (own_hidden, down_weight), name="down"
    )

    summed = call(
        join_kernel, struct((CHIPS, ROWS, COLS)), (own_out, passed, plain), name="join"
    )
    summed = exchange(summed, ("x", "mp"))
    lines = call(chip_sum_kernel, struct((DP, D // HEAD, HEAD)), (summed,), name="chip_sum")
    lines = exchange(lines, "dp")
    return call(final_kernel, struct((1, D)), (lines,), name="final")


def solution(mesh):
    fine = Mesh(mesh.devices.reshape(DP, NX, NC, MP), ("dp", "x", "core", "mp"))
    expert = ("x", "core")
    return jax.shard_map(
        body,
        mesh=fine,
        in_specs=(
            P("dp", expert),
            P(None, "dp", expert),
            P(expert, ("dp", "mp"), None, None, None),
            P(),
            P(),
            P(),
            P("dp", None),
            P(),
            P((*expert, "mp"), None),
            P(),
            P(),
            P(expert, None, ("dp", "mp")),
            P(expert, None, ("dp", "mp")),
            P(expert, ("dp", "mp"), None),
        ),
        out_specs=P(("dp", *expert, "mp"), None),
        check_vma=False,
    )
```

time: 120 us -> 119 us (level)
  blocking collectives: 104 us -> 90.5 us
  starting transfers between devices: 0.32 us -> 8.65 us
  waiting for transfers between devices: 5 us -> 8.67 us
  Pallas kernels: 8.46 us -> 10.8 us
  local copies, waits for them, and re-layouts: 2.24 us -> 0.04 us
    all_to_all x7 -> x6, blocking collectives: 104 us -> 90.5 us  [exchange(): return lax.all_to_all(array, axes, 0, 0, tiled=True)]
    all_to_all x0 -> x1, starting transfers between devices: none -> 8.47 us  [exchange(): return lax.all_to_all(array, axes, 0, 0, tiled=True)]
    all_to_all x0 -> x1, waiting for transfers between devices: none -> 5.3 us  [exchange(): return lax.all_to_all(array, axes, 0, 0, tiled=True)]
    pallas_call x12, Pallas kernels: 8.46 us -> 10.8 us  [call(): pl.pallas_call(kernel, out_shape=out_shape, in_specs=[anywhere if k in hb...]
    unnamed x22 -> x16, local copies, waits for them, and re-layouts: 2.24 us -> 0.04 us
    ppermute x3 -> x2, waiting for transfers between devices: 5 us -> 3.37 us  [swap(): return lax.ppermute(array, 'core', [(0, 1), (1, 0)])]
  transfers between devices with their start and end apart: 3 -> 3, of which waited for: 3 -> 3; matrix products, arithmetic and copies ran while one was open for 0% -> 0% of each run, Pallas kernels for 1% -> 3%
where the time goes in v4:
time: 119 us
  blocking collectives  90.5 us (76%)
  Pallas kernels  10.8 us (9%)
  waiting for transfers between devices  8.67 us (7%)
  starting transfers between devices  8.65 us (7%)
    all_to_all x6, blocking collectives, exchange(): return lax.all_to_all(array, axes, 0, 0, tiled=True)  90.5 us
    pallas_call x12, Pallas kernels, call(): pl.pallas_call(kernel, out_shape=out_shape, in_specs=[anywhere if k in hb...  10.8 us
    all_to_all x1, starting transfers between devices, exchange(): return lax.all_to_all(array, axes, 0, 0, tiled=True)  8.47 us
    all_to_all x1, waiting for transfers between devices, exchange(): return lax.all_to_all(array, axes, 0, 0, tiled=True)  5.3 us
    ppermute x2, waiting for transfers between devices, swap(): return lax.ppermute(array, 'core', [(0, 1), (1, 0)])  3.37 us
  transfers between devices with their start and end apart: 3, of which 3 were waited for; matrix products, arithmetic and copies ran while one was open for 0% of the time, Pallas kernels for 3%

profile of v4, /device:TPU:8, one launch (start us, length us, event | category | flops | bytes accessed | tf_op | source)
XLA Modules:
  0.0 118.8 jit_solution(8072639166239733516)
XLA Ops:
  0.0 1.6 %select.1.after = bf16[128,128]{1,0:T(8,128)(2,1)} custom-call(bf16[32,512]{1,0:T(8,128)(2,1)} %queries.3, s32[4,256]{1,0:T(4,128)} %bitcast.17), custom_call_target="tpu_custom_call" | custom-call | tf_op jit(solution)/shard_map/select/pallas_call | solution.py:304
  1.6 8.5 %all-to-all-start = ((bf16[8,16,128]{2,1,0:T(8,128)(2,1)}), bf16[8,16,128]{2,1,0:T(8,128)(2,1)S(1)}, u32[]{:S(2)}, u32[]{:S(2)}) async-start(bf16[8,16,128]{2,1,0:T(8,128)(2,1)} %bitcast.1), calls=%async_computation | async-start | bytes 65536 | tf_op jit(solution)/shard_map/all_to_all | solution.py:324
  10.1 2.7 %prepare.1 = (bf16[256,128]{1,0:T(8,128)(2,1)S(1)}, f32[256,128]{1,0:T(8,128)S(1)}, bf16[256,512]{1,0:T(8,128)(2,1)S(1)}, bf16[256,256]{1,0:T(8,128)(2,1)S(1)}, ...) custom-call(bf16[128,128]{1,0:T(8,128)(2,1)} %select.1.after, ...), custom_call_target="tpu_custom_call" | custom-call | tf_op jit(solution)/shard_map/prepare/pallas_call | solution.py:304
  12.8 5.3 %all-to-all-done = bf16[8,16,128]{2,1,0:T(8,128)(2,1)S(1)} async-done(((bf16[8,16,128]{2,1,0:T(8,128)(2,1)}), bf16[8,16,128]{2,1,0:T(8,128)(2,1)S(1)}, u32[]{:S(2)}, u32[]{:S(2)}) %all-to-all-start) | async-done | bytes 32800 | tf_op jit(solution)/shard_map/all_to_all | solution.py:324
  18.1 2.5 %attend.1 = bf16[256,128]{1,0:T(8,128)(2,1)S(1)} custom-call(bf16[128,128]{1,0:T(8,128)(2,1)S(1)} %bitcast.14, bf16[256,128]{1,0:T(8,128)(2,1)S(1)} %get-tuple-element.19.spread, f32[256,128]{1,0:T(8,128)S(1)} %get-tuple-element.20.live, bf16[256,512]{1,0:T(8,128)(2,1)S(1)} %get-tuple-element.21.gather, ...), custom_call_target="tpu_custom_call" | custom-call | tf_op jit(solution)/shard_map/attend/pallas_call | solution.py:304
  20.6 0.0 copy-start.4
  20.6 13.8 %all_to_all.35 = bf16[32,8,128]{2,1,0:T(8,128)(2,1)S(1)} all-to-all(bf16[32,8,128]{2,1,0:T(8,128)(2,1)S(1)} %bitcast.13), channel_id=1, replica_groups=mesh['dp'=8,'x'=4,'core'=2,'mp'=4] {'dp','mp'}, dimensions={0} | all-to-all | bytes 131072 | tf_op jit(solution)/shard_map/all_to_all | solution.py:324
  34.4 0.0 copy-start.2
  34.4 0.7 project.1
  35.1 13.5 %all_to_all.36.received = bf16[16,32,256]{2,1,0:T(8,128)(2,1)S(1)} all-to-all(bf16[16,32,256]{2,1,0:T(8,128)(2,1)S(1)} %project.1), channel_id=1, replica_groups=mesh['dp'=8,'x'=4,'core'=2,'mp'=4] {'x','mp'}, dimensions={0} | all-to-all | bytes 524288 | tf_op jit(solution)/shard_map/all_to_all | solution.py:324
  48.7 0.1 collective-permute-start
  48.8 1.2 collective-permute-done.theirs
  50.0 12.0 %all_to_all.37 = bf16[8,32,256]{2,1,0:T(8,128)(2,1)S(1)} all-to-all(bf16[8,32,256]{2,1,0:T(8,128)(2,1)S(1)} %get-tuple-element.26), channel_id=1, replica_groups=mesh['dp'=8,'x'=4,'core'=2,'mp'=4] {'dp'}, dimensions={0} | all-to-all | bytes 262144 | tf_op jit(solution)/shard_map/all_to_all | solution.py:324
  62.0 0.2 pick.1
  62.3 19.8 %all_to_all.38.rows = bf16[16,128,256]{2,1,0:T(8,128)(2,1)S(1)} all-to-all(bf16[16,128,256]{2,1,0:T(8,128)(2,1)S(1)} %pick.1), channel_id=1, replica_groups=mesh['dp'=8,'x'=4,'core'=2,'mp'=4] {'x','mp'}, dimensions={0} | all-to-all | bytes 2097152 | tf_op jit(solution)/shard_map/all_to_all | solution.py:324
  82.0 1.4 %hidden.1 = (bf16[16,128,256]{2,1,0:T(8,128)(2,1)S(1)}, bf16[128,256]{1,0:T(8,128)(2,1)S(1)}) custom-call(bf16[16,128,256]{2,1,0:T(8,128)(2,1)S(1)} %all_to_all.38.rows, f32[1,4096]{1,0:T(1,128)S(1)} %bitcast.16, bf16[1,4096,256]{2,1,0:T(8,128)(2,1)S(1)} %copy-done.1, bf16[1,4096,256]{2,1,0:T(8,128)(2,1)S(1)} %copy-done.2, ...), custom_call_target="tpu_custom_call" | custom-call | tf_op jit(solution)/shard_map/hidden/pallas_call | solution.py:304
  83.4 0.1 collective-permute-start.1
  83.5 0.4 down.1.mine
  84.0 2.2 %collective-permute-done.1.theirs = bf16[16,128,256]{2,1,0:T(8,128)(2,1)S(1)} collective-permute-done((bf16[16,128,256]{2,1,0:T(8,128)(2,1)S(1)}, bf16[16,128,256]{2,1,0:T(8,128)(2,1)S(1)}, u32[]{:S(2)}, u32[]{:S(2)}) %collective-permute-start.1) | collective-permute-done | bytes 1048608 | tf_op jit(solution)/shard_map/ppermute | solution.py:328
  86.1 0.4 join.1
  86.5 20.7 %all_to_all.39.received = bf16[16,128,256]{2,1,0:T(8,128)(2,1)S(1)} all-to-all(bf16[16,128,256]{2,1,0:T(8,128)(2,1)S(1)} %join.1), channel_id=1, replica_groups=mesh['dp'=8,'x'=4,'core'=2,'mp'=4] {'x','mp'}, dimensions={0} | all-to-all | bytes 2097152 | tf_op jit(solution)/shard_map/all_to_all | solution.py:324
  107.2 0.2 chip_sum.1
  107.4 10.8 %all_to_all.40.received = bf16[8,32,128]{2,1,0:T(8,128)(2,1)S(1)} all-to-all(bf16[8,32,128]{2,1,0:T(8,128)(2,1)S(1)} %chip_sum.1), channel_id=1, replica_groups=mesh['dp'=8,'x'=4,'core'=2,'mp'=4] {'dp'}, dimensions={0} | all-to-all | bytes 131072 | tf_op jit(solution)/shard_map/all_to_all | solution.py:324
  118.2 0.6 final.1
  (16 shorter events, 0.1 us)
Async XLA Ops:
  1.6 16.5 %all-to-all-start = ((bf16[8,16,128]{2,1,0:T(8,128)(2,1)}), bf16[8,16,128]{2,1,0:T(8,128)(2,1)S(1)}, u32[]{:S(2)}, u32[]{:S(2)}) async-start(bf16[8,16,128]{2,1,0:T(8,128)(2,1)} %bitcast.1), calls=%async_computation | async-start | bytes 65536 | tf_op jit(solution)/shard_map/all_to_all | solution.py:324
  18.1 16.3 %copy-start.3 = (bf16[128,4096]{1,0:T(8,128)(2,1)S(1)}, bf16[128,4096]{1,0:T(8,128)(2,1)}, u32[]{:S(2)}) copy-start(bf16[128,4096]{1,0:T(8,128)(2,1)} %weight.3) | copy-start | bytes 3145732
  18.1 16.3 %copy-start.5 = (bf16[32,512]{1,0:T(8,128)(2,1)S(1)}, bf16[32,512]{1,0:T(8,128)(2,1)}, u32[]{:S(2)}) copy-start(bf16[32,512]{1,0:T(8,128)(2,1)} %queries.3) | copy-start | bytes 98308
  18.1 16.3 %copy-start.7 = (bf16[2,32,128]{2,1,0:T(8,128)(2,1)S(1)}, bf16[2,32,128]{2,1,0:T(8,128)(2,1)}, u32[]{:S(2)}) copy-start(bf16[2,32,128]{2,1,0:T(8,128)(2,1)} %fresh.1) | copy-start | bytes 49156
  20.6 29.4 %copy-start.4 = (bf16[32,4096]{1,0:T(8,128)(2,1)S(1)}, bf16[32,4096]{1,0:T(8,128)(2,1)}, u32[]{:S(2)}) copy-start(bf16[32,4096]{1,0:T(8,128)(2,1)} %tokens.1) | copy-start | bytes 786436
  20.6 29.3 %copy-start.6 = (f32[4096]{0:T(1024)S(1)}, f32[4096]{0:T(1024)}, u32[]{:S(2)}) copy-start(f32[4096]{0:T(1024)} %param.21) | copy-start | bytes 49156
  34.4 47.6 %copy-start.2 = (bf16[1,4096,256]{2,1,0:T(8,128)(2,1)S(1)}, bf16[1,4096,256]{2,1,0:T(8,128)(2,1)}, u32[]{:S(2)}) copy-start(bf16[1,4096,256]{2,1,0:T(8,128)(2,1)} %up.1) | copy-start | bytes 6291460
  48.6 33.4 %copy-start.1 = (bf16[1,4096,256]{2,1,0:T(8,128)(2,1)S(1)}, bf16[1,4096,256]{2,1,0:T(8,128)(2,1)}, u32[]{:S(2)}) copy-start(bf16[1,4096,256]{2,1,0:T(8,128)(2,1)} %gate.1) | copy-start | bytes 6291460
  48.7 33.4 %copy-start = (bf16[1,256,4096]{2,1,0:T(8,128)(2,1)S(1)}, bf16[1,256,4096]{2,1,0:T(8,128)(2,1)}, u32[]{:S(2)}) copy-start(bf16[1,256,4096]{2,1,0:T(8,128)(2,1)} %weight.5) | copy-start | bytes 6291460
  48.7 1.3 %collective-permute-start = (bf16[32,256]{1,0:T(8,128)(2,1)S(1)}, bf16[32,256]{1,0:T(8,128)(2,1)S(1)}, u32[]{:S(2)}, u32[]{:S(2)}) collective-permute-start(bf16[32,256]{1,0:T(8,128)(2,1)S(1)} %get-tuple-element.25), channel_id=1, source_target_pairs={{0,4},{4,0},{1,5},{5,1},{2,6},{6,2},{3,7},{7,3},{8,12},{12,8},{9,1... | collective-permute-start | bytes 49160 | tf_op jit(solution)/shard_map/ppermute | solution.py:328
  83.4 2.7 %collective-permute-start.1 = (bf16[16,128,256]{2,1,0:T(8,128)(2,1)S(1)}, bf16[16,128,256]{2,1,0:T(8,128)(2,1)S(1)}, u32[]{:S(2)}, u32[]{:S(2)}) collective-permute-start(bf16[16,128,256]{2,1,0:T(8,128)(2,1)S(1)} %get-tuple-element.31), channel_id=1, source_target_pairs={{0,4},{4,0},{1,5},{5,1},{2,6},{6,2},{3,7},{7,3},{8,12},{12,8},{9,1... | collective-permute-start | bytes 3145736 | tf_op jit(solution)/shard_map/ppermute | solution.py:328

commit v5 on v4

--- a/solution.py
+++ b/solution.py
@@ -224,16 +224,14 @@
         out[k] = dot(attended, weight[:, k * COLS : (k + 1) * COLS]).astype(bf16)
 
 
-def sum_kernel(received, mine, sent):
-    summed = jnp.sum(received[...].astype(f32), axis=0)
-    mine[...] = summed
-    sent[...] = summed.astype(bf16)
-
-
-def residual_kernel(mine, theirs, tokens, gain, out, plain):
+def core_sum_kernel(mine, theirs, out):
+    out[...] = (mine[...].astype(f32) + theirs[...].astype(f32)).astype(bf16)
+
+
+def residual_kernel(received, tokens, gain, out, plain):
     chip = lax.axis_index("x") * MP + lax.axis_index("mp")
     cols = pl.ds(pl.multiple_of(chip * COLS, COLS), COLS)
-    total = mine[...] + theirs[...].astype(f32) + tokens[:, cols].astype(f32)
+    total = jnp.sum(received[...].astype(f32), axis=0) + tokens[:, cols].astype(f32)
     gained = (total * gain[:, cols]).astype(bf16)
     out[...] = jnp.broadcast_to(gained[None], (DP, SEQ, COLS))
     lines = total.reshape(NX, NC * MP, COLS)
@@ -400,18 +398,18 @@
         (parts, queries, fresh_entries, order, out_weight),
         name="project",
     )
+    projected = call(
+        core_sum_kernel,
+        struct((CHIPS, SEQ, COLS)),
+        (projected, swap(projected)),
+        name="core_sum",
+    )
     projected = exchange(projected, ("x", "mp"))
-    mine, sent = call(
-        sum_kernel,
-        (struct((SEQ, COLS), f32), struct((SEQ, COLS))),
-        (projected,),
-        name="sum_heads",
-    )
 
     gained, plain = call(
         residual_kernel,
         (struct((DP, SEQ, COLS)), struct((NX, NC * MP, COLS), f32)),
-        (mine, swap(sent), tokens, gain),
+        (projected, tokens, gain),
         name="residual",
     )
     gained = exchange(gained, "dp").reshape(TOTAL, COLS)

time: 119 us -> 119 us (level)
  no operation moved by 1% of the time
where the time goes in v5:
time: 119 us; the launch traced here: 118 us
  blocking collectives  89.4 us (75%)
  Pallas kernels  10.9 us (9%)
  waiting for transfers between devices  9.02 us (8%)
  starting transfers between devices  8.65 us (7%)
    all_to_all x6, blocking collectives, exchange(): return lax.all_to_all(array, axes, 0, 0, tiled=True)  89.4 us
    pallas_call x12, Pallas kernels, call(): pl.pallas_call(kernel, out_shape=out_shape, in_specs=[anywhere if k in hb...  10.9 us
    all_to_all x1, starting transfers between devices, exchange(): return lax.all_to_all(array, axes, 0, 0, tiled=True)  8.47 us
    all_to_all x1, waiting for transfers between devices, exchange(): return lax.all_to_all(array, axes, 0, 0, tiled=True)  5.3 us
    ppermute x2, waiting for transfers between devices, swap(): return lax.ppermute(array, 'core', [(0, 1), (1, 0)])  3.72 us
  transfers between devices with their start and end apart: 3, of which 3 were waited for; matrix products, arithmetic and copies ran while one was open for 0% of the time, Pallas kernels for 3%

profile of v5, /device:TPU:8, one launch (start us, length us, event | category | flops | bytes accessed | tf_op | source)
XLA Modules:
  0.0 118.1 jit_solution(17259157785543915836)
XLA Ops:
  0.0 1.6 %select.1.after = bf16[128,128]{1,0:T(8,128)(2,1)} custom-call(bf16[32,512]{1,0:T(8,128)(2,1)} %queries.3, s32[4,256]{1,0:T(4,128)} %bitcast.17), custom_call_target="tpu_custom_call" | custom-call | tf_op jit(solution)/shard_map/select/pallas_call | solution.py:302
  1.6 8.5 %all-to-all-start = ((bf16[8,16,128]{2,1,0:T(8,128)(2,1)}), bf16[8,16,128]{2,1,0:T(8,128)(2,1)S(1)}, u32[]{:S(2)}, u32[]{:S(2)}) async-start(bf16[8,16,128]{2,1,0:T(8,128)(2,1)} %bitcast.1), calls=%async_computation | async-start | bytes 65536 | tf_op jit(solution)/shard_map/all_to_all | solution.py:322
  10.1 2.7 %prepare.1 = (bf16[256,128]{1,0:T(8,128)(2,1)S(1)}, f32[256,128]{1,0:T(8,128)S(1)}, bf16[256,512]{1,0:T(8,128)(2,1)S(1)}, bf16[256,256]{1,0:T(8,128)(2,1)S(1)}, ...) custom-call(bf16[128,128]{1,0:T(8,128)(2,1)} %select.1.after, ...), custom_call_target="tpu_custom_call" | custom-call | tf_op jit(solution)/shard_map/prepare/pallas_call | solution.py:302
  12.8 5.3 %all-to-all-done = bf16[8,16,128]{2,1,0:T(8,128)(2,1)S(1)} async-done(((bf16[8,16,128]{2,1,0:T(8,128)(2,1)}), bf16[8,16,128]{2,1,0:T(8,128)(2,1)S(1)}, u32[]{:S(2)}, u32[]{:S(2)}) %all-to-all-start) | async-done | bytes 32800 | tf_op jit(solution)/shard_map/all_to_all | solution.py:322
  18.1 2.5 %attend.1 = bf16[256,128]{1,0:T(8,128)(2,1)S(1)} custom-call(bf16[128,128]{1,0:T(8,128)(2,1)S(1)} %bitcast.14, bf16[256,128]{1,0:T(8,128)(2,1)S(1)} %get-tuple-element.17.spread, f32[256,128]{1,0:T(8,128)S(1)} %get-tuple-element.18.live, bf16[256,512]{1,0:T(8,128)(2,1)S(1)} %get-tuple-element.19.gather, ...), custom_call_target="tpu_custom_call" | custom-call | tf_op jit(solution)/shard_map/attend/pallas_call | solution.py:302
  20.6 13.8 %all_to_all.35 = bf16[32,8,128]{2,1,0:T(8,128)(2,1)S(1)} all-to-all(bf16[32,8,128]{2,1,0:T(8,128)(2,1)S(1)} %bitcast.13), channel_id=1, replica_groups=mesh['dp'=8,'x'=4,'core'=2,'mp'=4] {'dp','mp'}, dimensions={0} | all-to-all | bytes 131072 | tf_op jit(solution)/shard_map/all_to_all | solution.py:322
  34.4 0.7 project.1.mine
  35.1 0.1 collective-permute-start
  35.2 1.5 %collective-permute-done.theirs = bf16[16,32,256]{2,1,0:T(8,128)(2,1)S(1)} collective-permute-done((bf16[16,32,256]{2,1,0:T(8,128)(2,1)S(1)}, bf16[16,32,256]{2,1,0:T(8,128)(2,1)S(1)}, u32[]{:S(2)}, u32[]{:S(2)}) %collective-permute-start) | collective-permute-done | bytes 262176 | tf_op jit(solution)/shard_map/ppermute | solution.py:326
  36.8 0.1 core_sum.1
  36.8 13.8 %all_to_all.36.received = bf16[16,32,256]{2,1,0:T(8,128)(2,1)S(1)} all-to-all(bf16[16,32,256]{2,1,0:T(8,128)(2,1)S(1)} %core_sum.1), channel_id=1, replica_groups=mesh['dp'=8,'x'=4,'core'=2,'mp'=4] {'x','mp'}, dimensions={0} | all-to-all | bytes 524288 | tf_op jit(solution)/shard_map/all_to_all | solution.py:322
  50.7 0.1 residual.1
  50.7 11.7 %all_to_all.37 = bf16[8,32,256]{2,1,0:T(8,128)(2,1)S(1)} all-to-all(bf16[8,32,256]{2,1,0:T(8,128)(2,1)S(1)} %get-tuple-element.22), channel_id=1, replica_groups=mesh['dp'=8,'x'=4,'core'=2,'mp'=4] {'dp'}, dimensions={0} | all-to-all | bytes 262144 | tf_op jit(solution)/shard_map/all_to_all | solution.py:322
  62.5 0.2 pick.1
  62.7 18.7 %all_to_all.38.rows = bf16[16,128,256]{2,1,0:T(8,128)(2,1)S(1)} all-to-all(bf16[16,128,256]{2,1,0:T(8,128)(2,1)S(1)} %pick.1), channel_id=1, replica_groups=mesh['dp'=8,'x'=4,'core'=2,'mp'=4] {'x','mp'}, dimensions={0} | all-to-all | bytes 2097152 | tf_op jit(solution)/shard_map/all_to_all | solution.py:322
  81.4 1.4 %hidden.1 = (bf16[16,128,256]{2,1,0:T(8,128)(2,1)S(1)}, bf16[128,256]{1,0:T(8,128)(2,1)S(1)}) custom-call(bf16[16,128,256]{2,1,0:T(8,128)(2,1)S(1)} %all_to_all.38.rows, f32[1,4096]{1,0:T(1,128)S(1)} %bitcast.16, bf16[1,4096,256]{2,1,0:T(8,128)(2,1)S(1)} %copy-done.1, bf16[1,4096,256]{2,1,0:T(8,128)(2,1)S(1)} %copy-done.2, ...), custom_call_target="tpu_custom_call" | custom-call | tf_op jit(solution)/shard_map/hidden/pallas_call | solution.py:302
  82.8 0.1 collective-permute-start.1
  82.9 0.4 down.1.mine
  83.3 2.2 %collective-permute-done.1.theirs = bf16[16,128,256]{2,1,0:T(8,128)(2,1)S(1)} collective-permute-done((bf16[16,128,256]{2,1,0:T(8,128)(2,1)S(1)}, bf16[16,128,256]{2,1,0:T(8,128)(2,1)S(1)}, u32[]{:S(2)}, u32[]{:S(2)}) %collective-permute-start.1) | collective-permute-done | bytes 1048608 | tf_op jit(solution)/shard_map/ppermute | solution.py:326
  85.5 0.4 join.1
  85.9 20.6 %all_to_all.39.received = bf16[16,128,256]{2,1,0:T(8,128)(2,1)S(1)} all-to-all(bf16[16,128,256]{2,1,0:T(8,128)(2,1)S(1)} %join.1), channel_id=1, replica_groups=mesh['dp'=8,'x'=4,'core'=2,'mp'=4] {'x','mp'}, dimensions={0} | all-to-all | bytes 2097152 | tf_op jit(solution)/shard_map/all_to_all | solution.py:322
  106.6 0.2 chip_sum.1
  106.8 10.8 %all_to_all.40.received = bf16[8,32,128]{2,1,0:T(8,128)(2,1)S(1)} all-to-all(bf16[8,32,128]{2,1,0:T(8,128)(2,1)S(1)} %chip_sum.1), channel_id=1, replica_groups=mesh['dp'=8,'x'=4,'core'=2,'mp'=4] {'dp'}, dimensions={0} | all-to-all | bytes 131072 | tf_op jit(solution)/shard_map/all_to_all | solution.py:322
  117.5 0.6 final.1
  (16 shorter events, 0.0 us)
Async XLA Ops:
  1.6 16.5 %all-to-all-start = ((bf16[8,16,128]{2,1,0:T(8,128)(2,1)}), bf16[8,16,128]{2,1,0:T(8,128)(2,1)S(1)}, u32[]{:S(2)}, u32[]{:S(2)}) async-start(bf16[8,16,128]{2,1,0:T(8,128)(2,1)} %bitcast.1), calls=%async_computation | async-start | bytes 65536 | tf_op jit(solution)/shard_map/all_to_all | solution.py:322
  18.1 16.3 %copy-start.3 = (bf16[128,4096]{1,0:T(8,128)(2,1)S(1)}, bf16[128,4096]{1,0:T(8,128)(2,1)}, u32[]{:S(2)}) copy-start(bf16[128,4096]{1,0:T(8,128)(2,1)} %weight.3) | copy-start | bytes 3145732
  18.1 16.3 %copy-start.5 = (bf16[32,512]{1,0:T(8,128)(2,1)S(1)}, bf16[32,512]{1,0:T(8,128)(2,1)}, u32[]{:S(2)}) copy-start(bf16[32,512]{1,0:T(8,128)(2,1)} %queries.3) | copy-start | bytes 98308
  18.1 16.3 %copy-start.7 = (bf16[2,32,128]{2,1,0:T(8,128)(2,1)S(1)}, bf16[2,32,128]{2,1,0:T(8,128)(2,1)}, u32[]{:S(2)}) copy-start(bf16[2,32,128]{2,1,0:T(8,128)(2,1)} %fresh.1) | copy-start | bytes 49156
  20.6 30.1 %copy-start.4 = (bf16[32,4096]{1,0:T(8,128)(2,1)S(1)}, bf16[32,4096]{1,0:T(8,128)(2,1)}, u32[]{:S(2)}) copy-start(bf16[32,4096]{1,0:T(8,128)(2,1)} %tokens.1) | copy-start | bytes 786436
  20.6 30.1 %copy-start.6 = (f32[4096]{0:T(1024)S(1)}, f32[4096]{0:T(1024)}, u32[]{:S(2)}) copy-start(f32[4096]{0:T(1024)} %param.21) | copy-start | bytes 49156
  34.4 47.0 %copy-start.2 = (bf16[1,4096,256]{2,1,0:T(8,128)(2,1)S(1)}, bf16[1,4096,256]{2,1,0:T(8,128)(2,1)}, u32[]{:S(2)}) copy-start(bf16[1,4096,256]{2,1,0:T(8,128)(2,1)} %up.1) | copy-start | bytes 6291460
  35.1 1.6 %collective-permute-start = (bf16[16,32,256]{2,1,0:T(8,128)(2,1)S(1)}, bf16[16,32,256]{2,1,0:T(8,128)(2,1)S(1)}, u32[]{:S(2)}, u32[]{:S(2)}) collective-permute-start(bf16[16,32,256]{2,1,0:T(8,128)(2,1)S(1)} %project.1.mine), channel_id=1, source_target_pairs={{0,4},{4,0},{1,5},{5,1},{2,6},{6,2},{3,7},{7,3},{8,12},{12,8},{9,1... | collective-permute-start | bytes 786440 | tf_op jit(solution)/shard_map/ppermute | solution.py:326
  50.7 30.7 %copy-start = (bf16[1,256,4096]{2,1,0:T(8,128)(2,1)S(1)}, bf16[1,256,4096]{2,1,0:T(8,128)(2,1)}, u32[]{:S(2)}) copy-start(bf16[1,256,4096]{2,1,0:T(8,128)(2,1)} %weight.5) | copy-start | bytes 6291460
  50.7 30.7 %copy-start.1 = (bf16[1,4096,256]{2,1,0:T(8,128)(2,1)S(1)}, bf16[1,4096,256]{2,1,0:T(8,128)(2,1)}, u32[]{:S(2)}) copy-start(bf16[1,4096,256]{2,1,0:T(8,128)(2,1)} %gate.1) | copy-start | bytes 6291460
  82.8 2.7 %collective-permute-start.1 = (bf16[16,128,256]{2,1,0:T(8,128)(2,1)S(1)}, bf16[16,128,256]{2,1,0:T(8,128)(2,1)S(1)}, u32[]{:S(2)}, u32[]{:S(2)}) collective-permute-start(bf16[16,128,256]{2,1,0:T(8,128)(2,1)S(1)} %get-tuple-element.27), channel_id=1, source_target_pairs={{0,4},{4,0},{1,5},{5,1},{2,6},{6,2},{3,7},{7,3},{8,12},{12,8},{9,1... | collective-permute-start | bytes 3145736 | tf_op jit(solution)/shard_map/ppermute | solution.py:326

commit v6 on v5

--- a/solution.py
+++ b/solution.py
@@ -5,12 +5,12 @@
 from jax.experimental.pallas import tpu as pltpu
 from jax.sharding import Mesh, PartitionSpec as P
 
+
 bf16 = jnp.bfloat16
 f32 = jnp.float32
 i32 = jnp.int32
 
 DP, NX, NC, MP = 8, 4, 2, 4
-EXPERTS = NX * NC
 HOLDERS = DP * MP
 PMAX = 4
 SEQ = 32
@@ -202,7 +202,7 @@
     out[...] = dot(gather[...], parts[...].astype(bf16)).astype(bf16)
 
 
-def project_kernel(received, queries, fresh, order, weight, out):
+def project_kernel(received, queries, fresh, order, weight, out, rows):
     head = pl.multiple_of(lax.axis_index("mp") * HEAD, HEAD)
     sorted_parts = dot(order[...], received[...])
     pages = [sorted_parts[j * SEQ : (j + 1) * SEQ] for j in range(PMAX)]
@@ -220,12 +220,21 @@
         total = total + (part[:, 64:65] + part[:, 96:97]) * factor
         weighted = weighted + page * factor
     attended = (weighted / total).astype(bf16)
-    for k in range(CHIPS):
+    rows[...] = attended
+    for k in range(CHIPS // 2):
         out[k] = dot(attended, weight[:, k * COLS : (k + 1) * COLS]).astype(bf16)
 
 
-def core_sum_kernel(mine, theirs, out):
-    out[...] = (mine[...].astype(f32) + theirs[...].astype(f32)).astype(bf16)
+def project_late_kernel(rows, weight, out):
+    for k in range(CHIPS // 2):
+        first = (CHIPS // 2 + k) * COLS
+        out[k] = dot(rows[...], weight[:, first : first + COLS]).astype(bf16)
+
+
+def core_sum_kernel(mine_a, mine_b, theirs_a, theirs_b, out):
+    for first, mine, theirs in ((0, mine_a, theirs_a), (CHIPS // 2, mine_b, theirs_b)):
+        total = mine[...].astype(f32) + theirs[...].astype(f32)
+        out[first : first + CHIPS // 2] = total.astype(bf16)
 
 
 def residual_kernel(received, tokens, gain, out, plain):
@@ -296,7 +305,7 @@
         out[:, k * HEAD : (k + 1) * HEAD] = summed[k : k + 1].astype(bf16)
 
 
-def call(kernel, out_shape, arrays, scratch=(), limit=8, hbm=(), name=None):
+def call(kernel, out_shape, arrays, scratch=(), limit=8, hbm=()):
     vmem = pl.BlockSpec(memory_space=pltpu.VMEM)
     anywhere = pl.BlockSpec(memory_space=pl.ANY)
     return pl.pallas_call(
@@ -306,7 +315,6 @@
         out_specs=jax.tree.map(lambda _: vmem, out_shape),
         scratch_shapes=scratch,
         compiler_params=pltpu.CompilerParams(vmem_limit_bytes=limit * 2**20),
-        name=name,
     )(*arrays)
 
 
@@ -347,10 +355,7 @@
 
     lines = DP * GROUPS * PMAX
     selected = call(
-        select_kernel,
-        struct((lines, HEAD)),
-        (in_hbm(queries), in_hbm(holders)),
-        name="select",
+        select_kernel, struct((lines, HEAD)), (in_hbm(queries), in_hbm(holders))
     )
     asked = exchange(selected.reshape(DP, GROUPS * PMAX, HEAD), "dp").reshape(lines, HEAD)
     spread, live, gather, order, picks, scatter, weights, early = call(
@@ -376,7 +381,6 @@
         ),
         scratch=[pltpu.SemaphoreType.DMA(())],
         hbm=(0, 6),
-        name="prepare",
     )
     parts = call(
         attend_kernel,
@@ -388,21 +392,21 @@
             pltpu.SemaphoreType.DMA((STEPS - EARLY,)),
         ],
         hbm=(5,),
-        name="attend",
     )
     parts = exchange(parts.reshape(HOLDERS, 8, HEAD), ("dp", "mp")).reshape(TOTAL, HEAD)
 
-    projected = call(
+    half = struct((CHIPS // 2, SEQ, COLS))
+    part_a, attended = call(
         project_kernel,
-        struct((CHIPS, SEQ, COLS)),
+        (half, struct((SEQ, HEAD))),
         (parts, queries, fresh_entries, order, out_weight),
-        name="project",
-    )
+    )
+    swapped_a = swap(part_a)
+    part_b = call(project_late_kernel, half, (attended, out_weight))
     projected = call(
         core_sum_kernel,
         struct((CHIPS, SEQ, COLS)),
-        (projected, swap(projected)),
-        name="core_sum",
+        (part_a, part_b, swapped_a, swap(part_b)),
     )
     projected = exchange(projected, ("x", "mp"))
 
@@ -410,29 +414,23 @@
         residual_kernel,
         (struct((DP, SEQ, COLS)), struct((NX, NC * MP, COLS), f32)),
         (projected, tokens, gain),
-        name="residual",
     )
     gained = exchange(gained, "dp").reshape(TOTAL, COLS)
-    picked = call(pick_kernel, struct((CHIPS, ROWS, COLS)), (gained, picks), name="pick")
+    picked = call(pick_kernel, struct((CHIPS, ROWS, COLS)), (gained, picks))
     rows = exchange(picked, ("x", "mp"))
     other_out, own_hidden = call(
         hidden_kernel,
         (struct((CHIPS, ROWS, COLS)), struct((ROWS, FF))),
         (rows, gain, gate_weight, up_weight, scatter, weights, down_weight),
-        name="hidden",
     )
     passed = swap(other_out)
-    own_out = call(
-        down_kernel, struct((CHIPS, ROWS, COLS)), (own_hidden, down_weight), name="down"
-    )
-
-    summed = call(
-        join_kernel, struct((CHIPS, ROWS, COLS)), (own_out, passed, plain), name="join"
-    )
+    own_out = call(down_kernel, struct((CHIPS, ROWS, COLS)), (own_hidden, down_weight))
+
+    summed = call(join_kernel, struct((CHIPS, ROWS, COLS)), (own_out, passed, plain))
     summed = exchange(summed, ("x", "mp"))
-    lines = call(chip_sum_kernel, struct((DP, D // HEAD, HEAD)), (summed,), name="chip_sum")
+    lines = call(chip_sum_kernel, struct((DP, D // HEAD, HEAD)), (summed,))
     lines = exchange(lines, "dp")
-    return call(final_kernel, struct((1, D)), (lines,), name="final")
+    return call(final_kernel, struct((1, D)), (lines,))
 
 
 def solution(mesh):

time: 119 us -> 119 us (level)
    ppermute x2 -> x3, waiting for transfers between devices: 3.72 us -> 3.22 us  [swap(): return lax.ppermute(array, 'core', [(0, 1), (1, 0)])]
    pallas_call x12 -> x13, Pallas kernels: 10.9 us -> 11 us  [call(): pl.pallas_call(kernel, out_shape=out_shape, in_specs=[anywhere if k in hb...]
  transfers between devices with their start and end apart: 3 -> 4, of which waited for: 3 -> 4; matrix products, arithmetic and copies ran while one was open for 0% -> 0% of each run, Pallas kernels for 3% -> 3%
where the time goes in v6:
time: 119 us
  blocking collectives  89.9 us (76%)
  Pallas kernels  11 us (9%)
  starting transfers between devices  9.15 us (8%)
  waiting for transfers between devices  8.52 us (7%)
    all_to_all x6, blocking collectives, exchange(): return lax.all_to_all(array, axes, 0, 0, tiled=True)  89.9 us
    pallas_call x13, Pallas kernels, call(): pl.pallas_call(kernel, out_shape=out_shape, in_specs=[anywhere if k in hb...  11 us
    all_to_all x1, starting transfers between devices, exchange(): return lax.all_to_all(array, axes, 0, 0, tiled=True)  8.47 us
    all_to_all x1, waiting for transfers between devices, exchange(): return lax.all_to_all(array, axes, 0, 0, tiled=True)  5.3 us
    ppermute x3, waiting for transfers between devices, swap(): return lax.ppermute(array, 'core', [(0, 1), (1, 0)])  3.22 us
  transfers between devices with their start and end apart: 4, of which 4 were waited for; matrix products, arithmetic and copies ran while one was open for 0% of the time, Pallas kernels for 3%

profile of v6, /device:TPU:8, one launch (start us, length us, event | category | flops | bytes accessed | tf_op | source)
XLA Modules:
  0.0 118.8 jit_solution(15178436442585135302)
XLA Ops:
  0.0 1.6 %shard_map.136.after = bf16[128,128]{1,0:T(8,128)(2,1)} custom-call(bf16[32,512]{1,0:T(8,128)(2,1)} %queries.3, s32[4,256]{1,0:T(4,128)} %bitcast.17), custom_call_target="tpu_custom_call" | custom-call | tf_op jit(solution)/shard_map/pallas_call | solution.py:311
  1.6 8.5 %all-to-all-start = ((bf16[8,16,128]{2,1,0:T(8,128)(2,1)}), bf16[8,16,128]{2,1,0:T(8,128)(2,1)S(1)}, u32[]{:S(2)}, u32[]{:S(2)}) async-start(bf16[8,16,128]{2,1,0:T(8,128)(2,1)} %bitcast.1), calls=%async_computation | async-start | bytes 65536 | tf_op jit(solution)/shard_map/all_to_all | solution.py:330
  10.1 2.7 %shard_map.137 = (bf16[256,128]{1,0:T(8,128)(2,1)S(1)}, f32[256,128]{1,0:T(8,128)S(1)}, bf16[256,512]{1,0:T(8,128)(2,1)S(1)}, bf16[256,256]{1,0:T(8,128)(2,1)S(1...) custom-call(bf16[128,128]{1,0:T(8,128)(2,1)} %shard_map.136.after, ...), custom_call_target="tpu_custom_call" | custom-call | tf_op jit(solution)/shard_map/pallas_call | solution.py:311
  12.8 5.3 %all-to-all-done = bf16[8,16,128]{2,1,0:T(8,128)(2,1)S(1)} async-done(((bf16[8,16,128]{2,1,0:T(8,128)(2,1)}), bf16[8,16,128]{2,1,0:T(8,128)(2,1)S(1)}, u32[]{:S(2)}, u32[]{:S(2)}) %all-to-all-start) | async-done | bytes 32800 | tf_op jit(solution)/shard_map/all_to_all | solution.py:330
  18.1 2.5 %shard_map.138 = bf16[256,128]{1,0:T(8,128)(2,1)S(1)} custom-call(bf16[128,128]{1,0:T(8,128)(2,1)S(1)} %bitcast.14, bf16[256,128]{1,0:T(8,128)(2,1)S(1)} %get-tuple-element.19.spread, f32[256,128]{1,0:T(8,128)S(1)} %get-tuple-element.20.live, bf16[256,512]{1,0:T(8,128)(2,1)S(1)} %get-tuple-element.21.gather, ...), custom_call_target="tpu_custom_call" | custom-call | tf_op jit(solution)/shard_map/pallas_call | solution.py:311
  20.6 13.8 %all_to_all.35 = bf16[32,8,128]{2,1,0:T(8,128)(2,1)S(1)} all-to-all(bf16[32,8,128]{2,1,0:T(8,128)(2,1)S(1)} %bitcast.13), channel_id=1, replica_groups=mesh['dp'=8,'x'=4,'core'=2,'mp'=4] {'dp','mp'}, dimensions={0} | all-to-all | bytes 131072 | tf_op jit(solution)/shard_map/all_to_all | solution.py:330
  34.4 0.6 shard_map.139
  35.1 0.2 shard_map.140.mine_b
  35.4 0.5 collective-permute-start
  35.9 0.8 collective-permute-done.1.theirs_b
  36.7 0.2 collective-permute-done.theirs_a
  37.0 14.0 %all_to_all.36.received = bf16[16,32,256]{2,1,0:T(8,128)(2,1)S(1)} all-to-all(bf16[16,32,256]{2,1,0:T(8,128)(2,1)S(1)} %shard_map.141), channel_id=1, replica_groups=mesh['dp'=8,'x'=4,'core'=2,'mp'=4] {'x','mp'}, dimensions={0} | all-to-all | bytes 524288 | tf_op jit(solution)/shard_map/all_to_all | solution.py:330
  51.0 11.7 %all_to_all.37 = bf16[8,32,256]{2,1,0:T(8,128)(2,1)S(1)} all-to-all(bf16[8,32,256]{2,1,0:T(8,128)(2,1)S(1)} %get-tuple-element.26), channel_id=1, replica_groups=mesh['dp'=8,'x'=4,'core'=2,'mp'=4] {'dp'}, dimensions={0} | all-to-all | bytes 262144 | tf_op jit(solution)/shard_map/all_to_all | solution.py:330
  62.7 0.2 shard_map.143
  63.0 19.0 %all_to_all.38.rows = bf16[16,128,256]{2,1,0:T(8,128)(2,1)S(1)} all-to-all(bf16[16,128,256]{2,1,0:T(8,128)(2,1)S(1)} %shard_map.143), channel_id=1, replica_groups=mesh['dp'=8,'x'=4,'core'=2,'mp'=4] {'x','mp'}, dimensions={0} | all-to-all | bytes 2097152 | tf_op jit(solution)/shard_map/all_to_all | solution.py:330
  82.0 1.4 %shard_map.144 = (bf16[16,128,256]{2,1,0:T(8,128)(2,1)S(1)}, bf16[128,256]{1,0:T(8,128)(2,1)S(1)}) custom-call(bf16[16,128,256]{2,1,0:T(8,128)(2,1)S(1)} %all_to_all.38.rows, f32[1,4096]{1,0:T(1,128)S(1)} %bitcast.16, bf16[1,4096,256]{2,1,0:T(8,128)(2,1)S(1)} %copy-done.2, bf16[1,4096,256]{2,1,0:T(8,128)(2,1)S(1)} %copy-done.3, ...), custom_call_target="tpu_custom_call" | custom-call | tf_op jit(solution)/shard_map/pallas_call | solution.py:311
  83.3 0.1 collective-permute-start.2
  83.4 0.4 shard_map.145.mine
  83.9 2.2 %collective-permute-done.2.theirs = bf16[16,128,256]{2,1,0:T(8,128)(2,1)S(1)} collective-permute-done((bf16[16,128,256]{2,1,0:T(8,128)(2,1)S(1)}, bf16[16,128,256]{2,1,0:T(8,128)(2,1)S(1)}, u32[]{:S(2)}, u32[]{:S(2)}) %collective-permute-start.2) | collective-permute-done | bytes 1048608 | tf_op jit(solution)/shard_map/ppermute | solution.py:334
  86.1 0.4 shard_map.146
  86.5 20.7 %all_to_all.39.received = bf16[16,128,256]{2,1,0:T(8,128)(2,1)S(1)} all-to-all(bf16[16,128,256]{2,1,0:T(8,128)(2,1)S(1)} %shard_map.146), channel_id=1, replica_groups=mesh['dp'=8,'x'=4,'core'=2,'mp'=4] {'x','mp'}, dimensions={0} | all-to-all | bytes 2097152 | tf_op jit(solution)/shard_map/all_to_all | solution.py:330
  107.2 0.2 shard_map.147
  107.4 10.8 %all_to_all.40.received = bf16[8,32,128]{2,1,0:T(8,128)(2,1)S(1)} all-to-all(bf16[8,32,128]{2,1,0:T(8,128)(2,1)S(1)} %shard_map.147), channel_id=1, replica_groups=mesh['dp'=8,'x'=4,'core'=2,'mp'=4] {'dp'}, dimensions={0} | all-to-all | bytes 131072 | tf_op jit(solution)/shard_map/all_to_all | solution.py:330
  118.1 0.6 shard_map.148
  (19 shorter events, 0.2 us)
Async XLA Ops:
  1.6 16.5 %all-to-all-start = ((bf16[8,16,128]{2,1,0:T(8,128)(2,1)}), bf16[8,16,128]{2,1,0:T(8,128)(2,1)S(1)}, u32[]{:S(2)}, u32[]{:S(2)}) async-start(bf16[8,16,128]{2,1,0:T(8,128)(2,1)} %bitcast.1), calls=%async_computation | async-start | bytes 65536 | tf_op jit(solution)/shard_map/all_to_all | solution.py:330
  18.1 16.3 %copy-start.1 = (bf16[128,4096]{1,0:T(8,128)(2,1)S(1)}, bf16[128,4096]{1,0:T(8,128)(2,1)}, u32[]{:S(2)}) copy-start(bf16[128,4096]{1,0:T(8,128)(2,1)} %weight.5) | copy-start | bytes 3145732
  18.1 16.3 %copy-start.5 = (bf16[32,512]{1,0:T(8,128)(2,1)S(1)}, bf16[32,512]{1,0:T(8,128)(2,1)}, u32[]{:S(2)}) copy-start(bf16[32,512]{1,0:T(8,128)(2,1)} %queries.3) | copy-start | bytes 98308
  18.1 16.3 %copy-start.7 = (bf16[2,32,128]{2,1,0:T(8,128)(2,1)S(1)}, bf16[2,32,128]{2,1,0:T(8,128)(2,1)}, u32[]{:S(2)}) copy-start(bf16[2,32,128]{2,1,0:T(8,128)(2,1)} %fresh.1) | copy-start | bytes 49156
  20.6 30.3 %copy-start.4 = (bf16[32,4096]{1,0:T(8,128)(2,1)S(1)}, bf16[32,4096]{1,0:T(8,128)(2,1)}, u32[]{:S(2)}) copy-start(bf16[32,4096]{1,0:T(8,128)(2,1)} %tokens.1) | copy-start | bytes 786436
  20.6 30.3 %copy-start.6 = (f32[4096]{0:T(1024)S(1)}, f32[4096]{0:T(1024)}, u32[]{:S(2)}) copy-start(f32[4096]{0:T(1024)} %param.21) | copy-start | bytes 49156
  35.1 46.9 %copy-start.3 = (bf16[1,4096,256]{2,1,0:T(8,128)(2,1)S(1)}, bf16[1,4096,256]{2,1,0:T(8,128)(2,1)}, u32[]{:S(2)}) copy-start(bf16[1,4096,256]{2,1,0:T(8,128)(2,1)} %up.1) | copy-start | bytes 6291460
  35.3 1.4 %collective-permute-start.1 = (bf16[8,32,256]{2,1,0:T(8,128)(2,1)S(1)}, bf16[8,32,256]{2,1,0:T(8,128)(2,1)S(1)}, u32[]{:S(2)}, u32[]{:S(2)}) collective-permute-start(bf16[8,32,256]{2,1,0:T(8,128)(2,1)S(1)} %shard_map.140.mine_b), channel_id=1, source_target_pairs={{0,4},{4,0},{1,5},{5,1},{2,6},{6,2},{3,7},{7,3},{8,12},{12,8},{9,1... | collective-permute-start | bytes 393224 | tf_op jit(solution)/shard_map/ppermute | solution.py:334
  35.4 1.5 %collective-permute-start = (bf16[8,32,256]{2,1,0:T(8,128)(2,1)S(1)}, bf16[8,32,256]{2,1,0:T(8,128)(2,1)S(1)}, u32[]{:S(2)}, u32[]{:S(2)}) collective-permute-start(bf16[8,32,256]{2,1,0:T(8,128)(2,1)S(1)} %get-tuple-element.24.mine_a), channel_id=1, source_target_pairs={{0,4},{4,0},{1,5},{5,1},{2,6},{6,2},{3,7},{7,3},{8,12},{12,8},{9,1... | collective-permute-start | bytes 393224 | tf_op jit(solution)/shard_map/ppermute | solution.py:334
  50.9 31.0 %copy-start = (bf16[1,256,4096]{2,1,0:T(8,128)(2,1)S(1)}, bf16[1,256,4096]{2,1,0:T(8,128)(2,1)}, u32[]{:S(2)}) copy-start(bf16[1,256,4096]{2,1,0:T(8,128)(2,1)} %weight.7) | copy-start | bytes 6291460
  50.9 31.0 %copy-start.2 = (bf16[1,4096,256]{2,1,0:T(8,128)(2,1)S(1)}, bf16[1,4096,256]{2,1,0:T(8,128)(2,1)}, u32[]{:S(2)}) copy-start(bf16[1,4096,256]{2,1,0:T(8,128)(2,1)} %gate.1) | copy-start | bytes 6291460
  83.3 2.7 %collective-permute-start.2 = (bf16[16,128,256]{2,1,0:T(8,128)(2,1)S(1)}, bf16[16,128,256]{2,1,0:T(8,128)(2,1)S(1)}, u32[]{:S(2)}, u32[]{:S(2)}) collective-permute-start(bf16[16,128,256]{2,1,0:T(8,128)(2,1)S(1)} %get-tuple-element.31), channel_id=1, source_target_pairs={{0,4},{4,0},{1,5},{5,1},{2,6},{6,2},{3,7},{7,3},{8,12},{12,8},{9,1... | collective-permute-start | bytes 3145736 | tf_op jit(solution)/shard_map/ppermute | solution.py:334
